TPU v7x, 32 devices: a whole 2x2x4 slice. The times are simulated.
32 devices in a mesh: rep: 4 (over x, core), fsdp: 8 (over z, y).
Axes of the slice: x: 2, y: 2, z: 4, core: 2. Of those that a mesh axis runs over, the one named last changes fastest.
Arguments:
- layer_input: bfloat16 [2, 24576, 768], P(None, ('rep', 'fsdp')), may hold values from -6 to 6
- cotangent: bfloat16 [2, 24576, 768], P(None, ('rep', 'fsdp')), may hold values from -6 to 6
- lengths: int32 [2, 384], P(None, ('rep', 'fsdp')), may hold values from 0 to 320, as said below
- attn_gain: bfloat16 [768], P('fsdp'), may hold values from 0.5 to 1.5
- global_gain: bfloat16 [768], P('fsdp'), may hold values from 0.5 to 1.5
- query_weight: bfloat16 [768, 768], P('fsdp'), may hold values from -0.0546875 to 0.0546875
- key_weight: bfloat16 [768, 768], P('fsdp'), may hold values from -0.21875 to 0.21875
- value_weight: bfloat16 [768, 768], P('fsdp'), may hold values from -0.21875 to 0.21875
- out_weight: bfloat16 [768, 768], P('fsdp'), may hold values from -0.875 to 0.875
- ffn_gain: bfloat16 [768], P('fsdp'), may hold values from 0.5 to 1.5
- gate_weight: bfloat16 [768, 2048], P('fsdp'), may hold values from -0.21875 to 0.21875
- up_weight: bfloat16 [768, 2048], P('fsdp'), may hold values from -0.21875 to 0.21875
- down_weight: bfloat16 [2048, 768], P('fsdp'), may hold values from -0.125 to 0.125
Outputs:
- layer_output: bfloat16 [2, 24576, 768], P(None, ('rep', 'fsdp'))
- in_grad: bfloat16 [2, 24576, 768], P(None, ('rep', 'fsdp'))
- attn_gain_grad: float32 [768], P('fsdp')
- global_gain_grad: float32 [768], P('fsdp')
- query_grad: float32 [768, 768], P('fsdp')
- key_grad: float32 [768, 768], P('fsdp')
- value_grad: float32 [768, 768], P('fsdp')
- out_weight_grad: float32 [768, 768], P('fsdp')
- ffn_gain_grad: float32 [768], P('fsdp')
- gate_grad: float32 [768, 2048], P('fsdp')
- up_grad: float32 [768, 2048], P('fsdp')
- down_grad: float32 [2048, 768], P('fsdp')
Inputs may be any that keep to these rules, and one draw needn't show every extreme that they name: `lengths`: entry b of the 12 entries that one device holds for one micro-batch is 0 or the length of a sequence whose first token is in block b; a sequence of n tokens fills its first block and the next ceil(n / 64) - 1 blocks of the same device, ending before the next nonzero entry. A device's filled blocks come first. On the 4 devices of one fsdp index, sequences fill exactly 16 blocks of each micro-batch. Some sequence of every draw has 320 tokens.
All inputs are finite; a program needn't handle non-finite values.
Results may differ from a plain program's by a relative error of at most 0.03.
Values may be sent and summed in bfloat16 or wider, within the bound.
A program may use at most 256 MiB of HBM per device.

v0:
```python
from functools import partial

import jax
import jax.numpy as jnp
from jax import lax
from jax.experimental import pallas as pl
from jax.experimental.pallas import tpu as pltpu
from jax.sharding import PartitionSpec as P

H = 12
DH = 64
RADIUS = 127
GBLK = 16
BLK = 64
SLOTS = 10
MAX_SEQ_BLOCKS = 5
EPSILON = 1e-06
MASKED_SCORE = -1e30
MESH = pl.DeviceIdType.MESH
VMEM_LIMIT = 60 * 1024 * 1024
SEG_AT, LEN_AT, DEST_AT, TABLE_SIZE = 40, 80, 120, 256

ANY = pl.BlockSpec(memory_space=pl.ANY)
VMEM = pl.BlockSpec(memory_space=pltpu.VMEM)
SMEM = pl.BlockSpec(memory_space=pltpu.SMEM)


def grid_of(count):
    inner = 2 if count <= 8 else 4
    return count // inner, inner


def core_of(rank):
    return rank + 1 - 2 * (rank % 2)


def across_of(rank):
    return (rank + 2) % 4


def lens_kernel(lens_ref, all_ref, send_sem, recv_sem):
    rank = lax.axis_index("rep")
    barrier = pltpu.get_barrier_semaphore()
    for step in range(1, 4):
        pl.semaphore_signal(
            barrier, inc=1, device_id={"rep": (rank + step) % 4}, device_id_type=MESH
        )
    pl.semaphore_wait(barrier, 3)
    copies = []
    for step in range(1, 4):
        copy = pltpu.make_async_remote_copy(
            src_ref=lens_ref,
            dst_ref=all_ref.at[rank],
            send_sem=send_sem.at[step - 1],
            recv_sem=recv_sem.at[step - 1],
            device_id={"rep": (rank + step) % 4},
            device_id_type=MESH,
        )
        copy.start()
        copies.append(copy)
    all_ref[rank] = lens_ref[...]
    for copy in copies:
        copy.wait()


def table_kernel(micro, per_dev, lens_ref, tab_ref, order_ref, count_ref, load_ref):
    total = 4 * micro * per_dev

    def length_at(spot):
        return lens_ref[spot // (micro * per_dev), (spot // per_dev) % micro, spot % per_dev]

    def blocks_of(length):
        return (length + (BLK - 1)) // BLK

    def clear(spot, carry):
        tab_ref[spot] = -1
        return carry

    lax.fori_loop(0, TABLE_SIZE, clear, 0)
    for spot in range(4 * SLOTS):
        tab_ref[LEN_AT + spot] = 0
    for size in range(8):
        count_ref[size] = 0
    for dev in range(4):
        load_ref[dev] = 0

    def tally(spot, carry):
        length = length_at(spot)

        @pl.when(length > 0)
        def _():
            size = blocks_of(length)
            count_ref[size] = count_ref[size] + 1

        return carry

    lax.fori_loop(0, total, tally, 0)
    begin = 0
    for size in range(MAX_SEQ_BLOCKS, 0, -1):
        amount = count_ref[size]
        count_ref[size] = begin
        begin = begin + amount

    def place(spot, carry):
        length = length_at(spot)

        @pl.when(length > 0)
        def _():
            size = blocks_of(length)
            where = count_ref[size]
            order_ref[where] = spot
            count_ref[size] = where + 1

        return carry

    lax.fori_loop(0, total, place, 0)

    def assign(number, carry):
        spot = order_ref[number]
        length = length_at(spot)
        size = blocks_of(length)
        best = jnp.int32(0)
        low = load_ref[0]
        for dev in range(1, 4):
            here = load_ref[dev]
            best = jnp.where(here < low, dev, best)
            low = jnp.minimum(here, low)
        load_ref[best] = low + size

        def put(step, inner):
            slot = best * SLOTS + low + step
            tab_ref[slot] = spot + step
            tab_ref[SEG_AT + slot] = low
            tab_ref[LEN_AT + slot] = jnp.minimum(length - BLK * step, BLK)
            tab_ref[DEST_AT + spot + step] = slot
            return inner

        lax.fori_loop(0, size, put, 0)
        return carry

    lax.fori_loop(0, begin, assign, 0)


def deal_table(lengths):
    micro, per_dev = lengths.shape
    padded = jnp.pad(lengths, ((0, 8 - micro), (0, 128 - per_dev)))
    everyone = pl.pallas_call(
        lens_kernel,
        out_shape=jax.ShapeDtypeStruct((4, 8, 128), jnp.int32),
        in_specs=[VMEM],
        out_specs=VMEM,
        scratch_shapes=[pltpu.SemaphoreType.DMA((3,)), pltpu.SemaphoreType.DMA((3,))],
        compiler_params=pltpu.CompilerParams(collective_id=0, has_side_effects=True),
        name="lens_exchange",
    )(padded)
    return pl.pallas_call(
        partial(table_kernel, micro, per_dev),
        out_shape=jax.ShapeDtypeStruct((TABLE_SIZE,), jnp.int32),
        in_specs=[SMEM],
        out_specs=SMEM,
        scratch_shapes=[
            pltpu.SMEM((4 * micro * per_dev,), jnp.int32),
            pltpu.SMEM((8,), jnp.int32),
            pltpu.SMEM((4,), jnp.int32),
        ],
        name="deal_table",
    )(everyone)


def gather_kernel(
    outer, inner, splits, tab_ref, rows_ref, cots_ref, wa_ref, wb_ref, wc_ref,
    ga_ref, gb_ref, gc_ref, rows_out, cots_out,
    psend, precv, xsend, xrecv,
    z_send, z_recv, y_send, y_recv, c_send, c_recv, own_sem,
    p_send, p_recv, x_send, x_recv,
):
    rank = lax.axis_index("rep")
    spot = lax.axis_index("fsdp")
    core = rank % 2
    row, col = spot // inner, spot % inner
    count = outer * inner
    mate, across = core_of(rank), across_of(rank)
    pieces = [(wa_ref, ga_ref, start, width // 2) for start, width in splits]
    pieces.append((wb_ref, gb_ref, 0, wb_ref.shape[1] // 2))
    pieces.append((wc_ref, gc_ref, 0, None))
    halved = [number for number, piece in enumerate(pieces) if piece[3] is not None]

    barrier = pltpu.get_barrier_semaphore()
    neighbours = (
        (row + 1 < outer, {"fsdp": spot + inner}),
        (row > 0, {"fsdp": spot - inner}),
        (col + 1 < inner, {"fsdp": spot + 1}),
        (col > 0, {"fsdp": spot - 1}),
    )
    amount = jnp.int32(2)
    for there, device in neighbours:
        amount = amount + there.astype(jnp.int32)

        @pl.when(there)
        def _():
            pl.semaphore_signal(barrier, inc=1, device_id=device, device_id_type=MESH)

    for device in (mate, across):
        pl.semaphore_signal(barrier, inc=1, device_id={"rep": device}, device_id_type=MESH)
    pl.semaphore_wait(barrier, amount)

    def cut(ref, number):
        _, _, start, half = pieces[number]
        if half is None:
            return ref
        return ref.at[:, pl.ds(pl.multiple_of(start + core * half, 128), half)]

    def landed(number, shard):
        return cut(pieces[number][1].at[shard], number)

    late = []

    def send(there, src, dst, ssem, rsem, device):
        def describe():
            return pltpu.make_async_remote_copy(
                src_ref=src, dst_ref=dst, send_sem=ssem, recv_sem=rsem,
                device_id=device, device_id_type=MESH,
            )

        if there is None:
            describe().start()
            late.append((None, lambda: describe().wait_send()))
        else:
            @pl.when(there)
            def _():
                describe().start()

            late.append((there, lambda: describe().wait_send()))

    def arrive(number, shard, rsem):
        pltpu.make_async_remote_copy(
            src_ref=landed(number, shard), dst_ref=landed(number, shard),
            send_sem=own_sem.at[0], recv_sem=rsem,
            device_id={"rep": mate}, device_id_type=MESH,
        ).wait_recv()

    def both(first, second):
        return second if first is None else jnp.logical_and(first, second)

    def to_mate(there, number, shard):
        if number not in halved:
            return
        place = landed(number, shard)
        send(there, place, place, c_send.at[number, shard], c_recv.at[number, shard], {"rep": mate})

    def along_row(there, number, line, src):
        shard = line * inner + col
        place = landed(number, shard)
        src = place if src is None else src
        send(both(there, col + 1 < inner), src, place,
             y_send.at[0, 0, line, number], y_recv.at[0, 0, line, number], {"fsdp": spot + 1})
        send(both(there, col > 0), src, place,
             y_send.at[1, 0, line, number], y_recv.at[1, 0, line, number], {"fsdp": spot - 1})

    def from_row(there, number, line):
        for step in range(inner - 1):
            for way, source, onward, target in (
                (0, col - 1 - step, col + 1 < inner, spot + 1),
                (1, col + 1 + step, col > 0, spot - 1),
            ):
                here = jnp.logical_and(source >= 0, source < inner)
                here = both(there, here)
                shard = line * inner + source

                @pl.when(here)
                def _():
                    arrive(number, shard, y_recv.at[way, step, line, number])

                if step + 1 < inner - 1:
                    place = landed(number, shard)
                    send(both(here, onward), place, place,
                         y_send.at[way, step + 1, line, number],
                         y_recv.at[way, step + 1, line, number], {"fsdp": target})
                to_mate(here, number, shard)

    for number, piece in enumerate(pieces):
        src, place = cut(piece[0], number), landed(number, spot)
        send(row + 1 < outer, src, place, z_send.at[0, 0, number], z_recv.at[0, 0, number],
             {"fsdp": spot + inner})
        send(row > 0, src, place, z_send.at[1, 0, number], z_recv.at[1, 0, number],
             {"fsdp": spot - inner})
        along_row(None, number, row, src)
    own = [
        pltpu.make_async_copy(wa_ref, ga_ref.at[spot], own_sem.at[0]),
        pltpu.make_async_copy(wb_ref, gb_ref.at[spot], own_sem.at[1]),
        pltpu.make_async_copy(wc_ref, gc_ref.at[spot], own_sem.at[2]),
    ]
    for copy in own:
        copy.start()

    sources = (rows_ref, cots_ref)
    per_rank = rows_ref.shape[0]

    def picked(kind, target, slot):
        index = tab_ref[target * SLOTS + slot] - rank * per_rank
        mine = jnp.logical_and(index >= 0, index < per_rank)
        value = sources[kind][jnp.clip(index, 0, per_rank - 1)]
        return mine, value

    def mate_copy(kind, part):
        return pltpu.make_async_remote_copy(
            src_ref=psend.at[kind, part], dst_ref=precv.at[kind, part],
            send_sem=p_send.at[kind, part], recv_sem=p_recv.at[kind, part],
            device_id={"rep": mate}, device_id_type=MESH,
        )

    def across_copy(kind):
        return pltpu.make_async_remote_copy(
            src_ref=xsend.at[kind], dst_ref=xrecv.at[kind],
            send_sem=x_send.at[kind], recv_sem=x_recv.at[kind],
            device_id={"rep": across}, device_id_type=MESH,
        )

    for kind, part in ((0, 1), (1, 1), (0, 0), (1, 0)):
        target = mate if part == 0 else across_of(mate)

        def pack(slot, carry):
            mine, value = picked(kind, target, slot)
            psend[kind, part, slot] = jnp.where(mine, value, jnp.zeros_like(value))
            return carry

        lax.fori_loop(0, SLOTS, pack, 0)
        mate_copy(kind, part).start()
    for kind in range(2):
        mate_copy(kind, 1).wait_recv()

        def merge(slot, carry):
            mine, value = picked(kind, across, slot)
            xsend[kind, slot] = jnp.where(mine, value, precv[kind, 1, slot])
            return carry

        lax.fori_loop(0, SLOTS, merge, 0)
        across_copy(kind).start()

    def lines(step):
        return ((row - 1 - step >= 0, row - 1 - step, 0, row + 1 < outer, spot + inner),
                (row + 1 + step < outer, row + 1 + step, 1, row > 0, spot - inner))

    for step in range(outer - 1):
        for number in range(len(pieces)):
            for here, line, way, onward, target in lines(step):
                shard = line * inner + col

                @pl.when(here)
                def _():
                    arrive(number, shard, z_recv.at[way, step, number])

                if step + 1 < outer - 1:
                    place = landed(number, shard)
                    send(jnp.logical_and(here, onward), place, place,
                         z_send.at[way, step + 1, number], z_recv.at[way, step + 1, number],
                         {"fsdp": target})
                along_row(here, number, line, None)
                to_mate(here, number, shard)
        for number in range(len(pieces)):
            if step == 0:
                from_row(None, number, row)
            else:
                for here, line, *_ in lines(step - 1):
                    from_row(here, number, line)
    for number in range(len(pieces)):
        for here, line, *_ in lines(outer - 2):
            from_row(here, number, line)

    outs = (rows_out, cots_out)
    for kind in range(2):
        mate_copy(kind, 0).wait_recv()
        across_copy(kind).wait_recv()

        def finish(slot, carry):
            mine, value = picked(kind, rank, slot)
            outs[kind][slot] = jnp.where(mine, value, precv[kind, 0, slot] + xrecv[kind, slot])
            return carry

        lax.fori_loop(0, SLOTS, finish, 0)

    for shard in range(count):
        @pl.when(shard != spot)
        def _():
            for number in halved:
                other = pieces[number]
                view = other[1].at[shard].at[:, pl.ds(0, other[3])]
                pltpu.make_async_remote_copy(
                    src_ref=view, dst_ref=view, send_sem=own_sem.at[0],
                    recv_sem=c_recv.at[number, shard],
                    device_id={"rep": mate}, device_id_type=MESH,
                ).wait_recv()
    for there, finish_send in late:
        if there is None:
            finish_send()
        else:
            pl.when(there)(finish_send)
    for kind in range(2):
        for part in range(2):
            mate_copy(kind, part).wait_send()
        across_copy(kind).wait_send()
    for copy in own:
        copy.wait()


def gather_weights(count, splits, table, rows, cots, wa, wb, wc):
    outer, inner = grid_of(count)
    block = rows.shape[1:]
    kinds = len(splits) + 2
    dma = pltpu.SemaphoreType.DMA
    bf16 = jnp.bfloat16
    return pl.pallas_call(
        partial(gather_kernel, outer, inner, splits),
        out_shape=(
            jax.ShapeDtypeStruct((count,) + wa.shape, bf16),
            jax.ShapeDtypeStruct((count,) + wb.shape, bf16),
            jax.ShapeDtypeStruct((count,) + wc.shape, bf16),
            jax.ShapeDtypeStruct((SLOTS,) + block, bf16),
            jax.ShapeDtypeStruct((SLOTS,) + block, bf16),
        ),
        in_specs=[SMEM, VMEM, VMEM, VMEM, VMEM, VMEM],
        out_specs=(ANY, ANY, ANY, VMEM, VMEM),
        scratch_shapes=[
            pltpu.VMEM((2, 2, SLOTS) + block, bf16),
            pltpu.VMEM((2, 2, SLOTS) + block, bf16),
            pltpu.VMEM((2, SLOTS) + block, bf16),
            pltpu.VMEM((2, SLOTS) + block, bf16),
            dma((2, outer - 1, kinds)), dma((2, outer - 1, kinds)),
            dma((2, inner - 1, outer, kinds)), dma((2, inner - 1, outer, kinds)),
            dma((kinds, count)), dma((kinds, count)), dma((3,)),
            dma((2, 2)), dma((2, 2)), dma((2,)), dma((2,)),
        ],
        compiler_params=pltpu.CompilerParams(
            collective_id=1, has_side_effects=True, vmem_limit_bytes=VMEM_LIMIT
        ),
        name="gather_and_deal",
    )(table, rows, cots, wa, wb, wc)


def reduce_kernel(
    outer, inner, kinds, *refs
):
    grads, (y_ref, g_ref) = refs[:kinds], refs[kinds : kinds + 2]
    totals, (ry_ref, rg_ref) = refs[kinds + 2 : 2 * kinds + 2], refs[2 * kinds + 2 : 2 * kinds + 4]
    scratch = refs[2 * kinds + 4 :]
    mines, crecvs, yrecvs, zrecvs, xrecvs = (
        scratch[kinds * i : kinds * (i + 1)] for i in range(5)
    )
    (c_send, c_recv, m_sem, y_send, y_recv, z_send, z_recv, x_send, x_recv, f_send, f_recv,
     r_send, r_recv, q_sem) = scratch[5 * kinds :]
    rank = lax.axis_index("rep")
    spot = lax.axis_index("fsdp")
    core = rank % 2
    row, col = spot // inner, spot % inner
    mate, across = core_of(rank), across_of(rank)
    pieces = [(src, dst, 0, src.shape[3] // 2) for src, dst in zip(grads[:-1], totals)]
    pieces.append((grads[-1], totals[-1], 0, None))

    barrier = pltpu.get_barrier_semaphore()
    neighbours = (
        (row + 1 < outer, {"fsdp": spot + inner}),
        (row > 0, {"fsdp": spot - inner}),
        (col + 1 < inner, {"fsdp": spot + 1}),
        (col > 0, {"fsdp": spot - 1}),
    )
    amount = jnp.int32(2)
    for there, device in neighbours:
        amount = amount + there.astype(jnp.int32)

        @pl.when(there)
        def _():
            pl.semaphore_signal(barrier, inc=1, device_id=device, device_id_type=MESH)

    for device in (mate, across):
        pl.semaphore_signal(barrier, inc=1, device_id={"rep": device}, device_id_type=MESH)
    pl.semaphore_wait(barrier, amount)

    late = []

    def send(there, src, dst, ssem, rsem, device):
        def describe():
            return pltpu.make_async_remote_copy(
                src_ref=src, dst_ref=dst, send_sem=ssem, recv_sem=rsem,
                device_id=device, device_id_type=MESH,
            )

        if there is None:
            describe().start()
            late.append((None, lambda: describe().wait_send()))
        else:
            @pl.when(there)
            def _():
                describe().start()

            late.append((there, lambda: describe().wait_send()))

    def arrive(place, rsem):
        pltpu.make_async_remote_copy(
            src_ref=place, dst_ref=place, send_sem=q_sem.at[0], recv_sem=rsem,
            device_id={"rep": mate}, device_id_type=MESH,
        ).wait_recv()

    def columns(ref, number, which):
        _, _, start, half = pieces[number]
        if half is None:
            return ref
        cols = pl.ds(pl.multiple_of(start + which * half, 128), half)
        return ref.at[:, :, :, cols] if len(ref.shape) == 4 else ref.at[:, cols]

    order = list(range(kinds))
    loads = []
    for number in order:
        src = columns(pieces[number][0], number, 1 - core)
        send(None, src, crecvs[number], c_send.at[number], c_recv.at[number], {"rep": mate})
        load = pltpu.make_async_copy(
            columns(pieces[number][0], number, core), mines[number], m_sem.at[number]
        )
        load.start()
        loads.append(load)

    for kind, (src, dst) in enumerate(((y_ref, ry_ref), (g_ref, rg_ref))):
        send(None, src, dst.at[rank], r_send.at[kind, 0], r_recv.at[kind, 0], {"rep": across})
        send(None, src, dst.at[rank], r_send.at[kind, 1], r_recv.at[kind, 1], {"rep": mate})
        pltpu.make_async_copy(src, dst.at[rank], q_sem.at[kind + 1]).start()

    def slot_of(way, size, place, dest):
        if size == 2:
            return 0
        return dest - place if way == 0 else size - place + dest

    def line_sum(number, size, place, stride, buffer, view, ssem, rsem):
        for far in range(size - 1, 0, -1):
            for way in range(2):
                dest = far if way == 0 else size - 1 - far
                step = 1 if way == 0 else -1
                passes = place < dest if way == 0 else place > dest
                first = place == 0 if way == 0 else place == size - 1
                mine = view(dest)
                got = slot_of(way, size, place, dest)

                @pl.when(jnp.logical_and(passes, jnp.logical_not(first)))
                def _():
                    arrive(buffer.at[got], rsem.at[got, number])
                    mine[...] = mine[...] + buffer[got]

                put = slot_of(way, size, place + step, dest)
                send(passes, mine, buffer.at[put], ssem.at[way, dest, number], rsem.at[put, number],
                     {"fsdp": spot + step * stride})
        for way in range(2):
            has = place > 0 if way == 0 else place < size - 1
            got = slot_of(way, size, place, place)
            mine = view(place)

            @pl.when(has)
            def _():
                arrive(buffer.at[got], rsem.at[got, number])
                mine[...] = mine[...] + buffer[got]

    for number in order:
        loads[number].wait()
        arrive(crecvs[number], c_recv.at[number])
        mine, other = mines[number], crecvs[number]

        def add(index, carry):
            mine[index // inner, index % inner] = (
                mine[index // inner, index % inner] + other[index // inner, index % inner]
            )
            return carry

        lax.fori_loop(0, outer * inner, add, 0)
        if inner == 2:
            send(None, mine.at[:, 1 - col], yrecvs[number].at[0], y_send.at[0, 0, number],
                 y_recv.at[0, number], {"fsdp": spot + 1 - 2 * col})
    for kind, dst in enumerate((ry_ref, rg_ref)):
        place = dst.at[across]
        arrive(place, r_recv.at[kind, 0])
        send(None, place, place, r_send.at[kind, 2], r_recv.at[kind, 2], {"rep": mate})
    for number in order:
        mine = mines[number]
        if inner == 2:
            arrive(yrecvs[number].at[0], y_recv.at[0, number])
            buffer = yrecvs[number]

            def add(index, carry):
                mine[index, col] = mine[index, col] + buffer[0, index]
                return carry

            lax.fori_loop(0, outer, add, 0)
        else:
            line_sum(number, inner, col, 1, yrecvs[number], lambda dest: mine.at[:, dest],
                     y_send, y_recv)
        line_sum(number, outer, row, inner, zrecvs[number], lambda dest: mine.at[dest, col],
                 z_send, z_recv)
        send(None, mine.at[row, col], xrecvs[number], x_send.at[number], x_recv.at[number],
             {"rep": across})
    for number in order:
        arrive(xrecvs[number], x_recv.at[number])
        total = mines[number][row, col].astype(jnp.float32) + xrecvs[number][...].astype(jnp.float32)
        out, half = pieces[number][1], pieces[number][3]
        place = columns(out, number, core)
        place[...] = total
        if half is not None:
            send(None, place, place, f_send.at[number], f_recv.at[number], {"rep": mate})
    for number in order:
        if pieces[number][3] is not None:
            arrive(columns(pieces[number][1], number, 1 - core), f_recv.at[number])
    for kind, dst in enumerate((ry_ref, rg_ref)):
        arrive(dst.at[mate], r_recv.at[kind, 1])
        arrive(dst.at[across_of(mate)], r_recv.at[kind, 2])
        src = y_ref if kind == 0 else g_ref
        pltpu.make_async_copy(src, dst.at[rank], q_sem.at[kind + 1]).wait()
    for there, finish_send in late:
        if there is None:
            finish_send()
        else:
            pl.when(there)(finish_send)


def reduce_grads(count, grads, y_rows, g_rows):
    outer, inner = grid_of(count)
    kinds = len(grads)
    shapes = [(grad.shape[1], grad.shape[2] // 2, grad.dtype) for grad in grads[:-1]]
    shapes.append(grads[-1].shape[1:] + (grads[-1].dtype,))
    dma = pltpu.SemaphoreType.DMA
    y_slots = 1 if inner == 2 else inner + 1
    z_slots = 1 if outer == 2 else outer + 1
    scratch = []
    for lead in ((outer, inner), (outer, inner), (y_slots, outer), (z_slots,), ()):
        scratch += [pltpu.VMEM(lead + (a, b), dtype) for a, b, dtype in shapes]
    scratch += [
        dma((kinds,)), dma((kinds,)), dma((kinds,)),
        dma((2, inner, kinds)), dma((y_slots, kinds)),
        dma((2, outer, kinds)), dma((z_slots, kinds)),
        dma((kinds,)), dma((kinds,)), dma((kinds,)), dma((kinds,)),
        dma((2, 3)), dma((2, 3)), dma((3,)),
    ]
    return pl.pallas_call(
        partial(reduce_kernel, outer, inner, kinds),
        out_shape=tuple(jax.ShapeDtypeStruct(grad.shape[1:], jnp.float32) for grad in grads) + (
            jax.ShapeDtypeStruct((4,) + y_rows.shape, y_rows.dtype),
            jax.ShapeDtypeStruct((4,) + g_rows.shape, g_rows.dtype),
        ),
        in_specs=[ANY] * (kinds + 2),
        out_specs=(VMEM,) * kinds + (ANY, ANY),
        scratch_shapes=scratch,
        compiler_params=pltpu.CompilerParams(
            collective_id=2, has_side_effects=True, vmem_limit_bytes=VMEM_LIMIT
        ),
        name="reduce_and_return",
    )(*(grad.reshape((outer, inner) + grad.shape[1:]) for grad in grads), y_rows, g_rows)


def home_kernel(tab_ref, ry_ref, rg_ref, y_ref, g_ref):
    base = lax.axis_index("rep") * y_ref.shape[0]

    def fetch(block, carry):
        index = tab_ref[DEST_AT + base + block] if len(tab_ref.shape) == 1 else tab_ref[48, base + block]
        safe = jnp.maximum(index, 0)
        for src, dst in ((ry_ref, y_ref), (rg_ref, g_ref)):
            value = src[safe // SLOTS, safe % SLOTS]
            dst[block] = jnp.where(index >= 0, value, jnp.zeros_like(value))
        return carry

    lax.fori_loop(0, y_ref.shape[0], fetch, 0)


def bring_home(table, ry, rg, blocks):
    shape = jax.ShapeDtypeStruct((blocks,) + ry.shape[2:], ry.dtype)
    return pl.pallas_call(
        home_kernel,
        out_shape=(shape, shape),
        in_specs=[SMEM, VMEM, VMEM],
        out_specs=(VMEM, VMEM),
        compiler_params=pltpu.CompilerParams(vmem_limit_bytes=VMEM_LIMIT),
        name="place_rows",
    )(table, ry, rg)


D = H * DH
ROWS = SLOTS * BLK
SIDES = SLOTS * (BLK // GBLK)
SIDE_ROWS = 48
ALL_ROWS = ROWS + SIDE_ROWS
QT = 128
WIN = 384
TILES = ROWS // QT
QUAD = 256
FF_TILE = 256
GELU_C = 0.7978845608028654
GELU_A = 0.044715
F32, BF16 = jnp.float32, jnp.bfloat16


def mm(left, right):
    return lax.dot_general(left, right, (((1,), (0,)), ((), ())), preferred_element_type=F32)


def mm_cols(left, right):
    return lax.dot_general(left, right, (((1,), (1,)), ((), ())), preferred_element_type=F32)


def mm_rows(left, right):
    return lax.dot_general(left, right, (((0,), (0,)), ((), ())), preferred_element_type=F32)


def iota(shape, axis):
    return lax.broadcasted_iota(jnp.int32, shape, axis)


def pick_by(index, values, other):
    out = jnp.full(index.shape, other, jnp.int32)
    for number, value in enumerate(values):
        out = jnp.where(index == number, value, out)
    return out


def block_at(tab_ref, slot):
    return lax.rem(tab_ref[slot, 0], 128) - 1


def seg_at(tab_ref, slot):
    if len(tab_ref.shape) == 1:
        return tab_ref[SEG_AT + slot]
    return lax.div(tab_ref[slot, 0], 16384) - 1


def len_at(tab_ref, slot):
    if len(tab_ref.shape) == 1:
        return tab_ref[LEN_AT + slot]
    return lax.rem(lax.div(tab_ref[slot, 0], 128), 128)


def slot_info(tab_ref, rank):
    seg = [seg_at(tab_ref, rank * SLOTS + slot) for slot in range(SLOTS)]
    length = [len_at(tab_ref, rank * SLOTS + slot) for slot in range(SLOTS)]
    return seg, length


def valid_column(tab_ref, rank):
    _, length = slot_info(tab_ref, rank)
    row = iota((ROWS, 1), 0)
    return ((row % BLK) < pick_by(row // BLK, length, 0)).astype(F32)


def pooling(tab_ref, rank):
    _, length = slot_info(tab_ref, rank)
    row = iota((1, ROWS), 1)
    block = jnp.where((row % BLK) < pick_by(row // BLK, length, 0), row // GBLK, -1)
    return jnp.where(iota((SIDE_ROWS, ROWS), 0) == block, 1.0, 0.0).astype(BF16)


def key_segments(tab_ref, rank, first_block, index):
    blocks = WIN // BLK
    base = rank * SLOTS + first_block
    seg = [seg_at(tab_ref, base + step) for step in range(blocks)]
    length = [len_at(tab_ref, base + step) for step in range(blocks)]
    alive = (index % BLK) < pick_by(index // BLK, length, 0)
    return jnp.where(alive, pick_by(index // BLK, seg, -2), -2)


def side_segments(tab_ref, rank, index):
    seg, length = slot_info(tab_ref, rank)
    per = BLK // GBLK
    alive = (index % per) * GBLK < pick_by(index // per, length, 0)
    return jnp.where(alive, pick_by(index // per, seg, -2), -2)


def tile_bias(tab_ref, rank, tile, first_row, keys_axis):
    qs, ks, gs = ((QT, 1), (1, WIN), (1, SIDE_ROWS)) if keys_axis == 1 else ((1, QT), (WIN, 1), (SIDE_ROWS, 1))
    q_index = iota(qs, 1 - keys_axis)
    k_index = iota(ks, keys_axis)
    g_index = iota(gs, keys_axis)
    base = rank * SLOTS + tile * (QT // BLK)
    q_seg = pick_by(q_index // BLK, [seg_at(tab_ref, base + step) for step in range(QT // BLK)], -1)
    k_seg = key_segments(tab_ref, rank, first_row // BLK, k_index)
    g_seg = side_segments(tab_ref, rank, g_index)
    gap = (q_index + tile * QT) - (k_index + first_row)
    local = (jnp.abs(gap) <= RADIUS) & (q_seg == k_seg)
    return jnp.where(local, 0.0, MASKED_SCORE), jnp.where(q_seg == g_seg, 0.0, MASKED_SCORE)


def window_start(tile):
    return pl.multiple_of(jnp.clip(tile - 1, 0, TILES - WIN // QT) * QT, QT)


def head_stack(rows):
    lane = iota(rows.shape, 1) // DH
    zero = jnp.zeros_like(rows)
    return jnp.concatenate([jnp.where(lane == head, rows, zero) for head in range(QUAD // DH)], axis=0)


def head_merge(stacked):
    lane = iota((QT, QUAD), 1) // DH
    out = stacked[:QT]
    for head in range(1, QUAD // DH):
        out = jnp.where(lane == head, stacked[head * QT : (head + 1) * QT], out)
    return out


def gains_of(gc_ref):
    count = gc_ref.shape[0]
    part = D // count
    lane, column = iota((128, D), 0), iota((128, D), 1)
    total = None
    for shard in range(count):
        pick = jnp.where((column == lane + shard * part) & (lane < part), 1.0, 0.0).astype(BF16)
        term = mm(gc_ref[shard], pick)
        total = term if total is None else total + term
    return total


def three_way(value):
    high = value.astype(BF16)
    rest = value - high.astype(F32)
    middle = rest.astype(BF16)
    return high, middle, (rest - middle.astype(F32)).astype(BF16)


def spread_gain_grads(value, dc_ref):
    count = dc_ref.shape[0] if len(dc_ref.shape) == 3 else dc_ref.shape[0] * dc_ref.shape[1]
    part = D // count
    column, lane = iota((D, 128), 0), iota((D, 128), 1)
    parts = three_way(value)
    for shard in range(count):
        pick = jnp.where((column == lane + shard * part) & (lane < part), 1.0, 0.0).astype(BF16)
        place = dc_ref.at[shard] if len(dc_ref.shape) == 3 else dc_ref.at[shard // dc_ref.shape[1], shard % dc_ref.shape[1]]
        place[...] = mm(parts[0], pick) + mm(parts[1], pick) + mm(parts[2], pick)


def mean_square(value):
    return jnp.mean(value * value, axis=-1, keepdims=True)


def forward_norm(tab_ref, rank, x_ref, gains, n_ref):
    for tile in range(TILES):
        rows = pl.ds(tile * QT, QT)
        value = x_ref[rows, :].astype(F32)
        n_ref[rows, :] = (value * lax.rsqrt(mean_square(value) + EPSILON) * gains[0:1]).astype(BF16)
    side = mm(pooling(tab_ref, rank), n_ref[:ROWS, :])
    n_ref[ROWS:, :] = (side * lax.rsqrt(mean_square(side) + EPSILON) * gains[1:2]).astype(BF16)


def forward_project(n_ref, w_ref, qkv_ref):
    def step(tile, carry):
        cols = pl.ds(pl.multiple_of(tile * QUAD, QUAD), QUAD)
        qkv_ref[:, cols] = mm(n_ref[...], w_ref[:, cols]).astype(BF16)
        return carry

    lax.fori_loop(0, 3 * D // QUAD, step, 0)


def forward_attention(tab_ref, rank, qkv_ref, att_ref, lse_ref, begin, end):
    heads = QUAD // DH

    def step(tile, carry):
        first = window_start(tile)
        bias, side_bias = tile_bias(tab_ref, rank, tile, first, 1)
        rows = pl.ds(pl.multiple_of(tile * QT, QT), QT)
        window = pl.ds(first, WIN)
        lane = iota((QT, 128), 1)

        def four(quad, lse):
            low = pl.multiple_of(quad * QUAD, QUAD)
            cols, key_cols, value_cols = (pl.ds(low + number * D, QUAD) for number in range(3))
            query = head_stack(qkv_ref[rows, cols])
            scores = mm_cols(query, qkv_ref[window, key_cols])
            side_scores = mm_cols(query, qkv_ref[ROWS:, key_cols])
            local, sides, scale = [], [], []
            for head in range(heads):
                part = slice(head * QT, (head + 1) * QT)
                one = scores[part] + bias
                two = side_scores[part] + side_bias
                peak = jnp.maximum(
                    jnp.max(one, axis=-1, keepdims=True), jnp.max(two, axis=-1, keepdims=True)
                )
                one, two = jnp.exp(one - peak), jnp.exp(two - peak)
                total = jnp.sum(one, axis=-1, keepdims=True) + jnp.sum(two, axis=-1, keepdims=True)
                local.append(one.astype(BF16))
                sides.append(two.astype(BF16))
                scale.append(1.0 / total)
                lse = jnp.where(lane == quad * heads + head, peak + jnp.log(total), lse)
            mixed = mm(jnp.concatenate(local, axis=0), qkv_ref[window, value_cols])
            mixed = mixed + mm(jnp.concatenate(sides, axis=0), qkv_ref[ROWS:, value_cols])
            mixed = mixed * jnp.concatenate(scale, axis=0)
            att_ref[rows, cols] = head_merge(mixed).astype(BF16)
            return lse

        lse = lax.fori_loop(0, D // QUAD, four, jnp.zeros((QT, 128), F32))
        lse_ref[tile] = jnp.transpose(lse)[:16]
        return carry

    lax.fori_loop(begin, end, step, 0)


def feed_forward(tab_ref, rank, x_ref, cot_ref, att_ref, gains, w_ref, wb_ref,
                 y_ref, gh_ref, ga_ref, dg_ref, du_ref, db_ref, do_ref,
                 h1_ref, nt_ref, ntt_ref, gres_ref, h2_ref, gg_ref, gu_ref, gn_ref):
    hidden = wb_ref.shape[0]
    gate_at = w_ref.shape[1] - 2 * hidden
    out_at = gate_at - D
    valid = valid_column(tab_ref, rank)
    gain = gains[2:3]
    for tile in range(TILES):
        rows = pl.ds(tile * QT, QT)
        value = x_ref[rows, :].astype(F32) + mm(att_ref[rows, :], w_ref[:, out_at:gate_at])
        h1_ref[rows, :] = value
        normed = (value * lax.rsqrt(mean_square(value) + EPSILON) * gain).astype(BF16)
        nt_ref[rows, :] = normed
        ntt_ref[:, tile * QT : (tile + 1) * QT] = jnp.transpose(normed)
        gres_ref[rows, :] = (cot_ref[rows, :].astype(F32) * valid[tile * QT : (tile + 1) * QT]).astype(BF16)

    def inward(tile, carry):
        at = pl.multiple_of(tile * FF_TILE, FF_TILE)
        cols = pl.ds(at, FF_TILE)
        gate = mm(nt_ref[...], w_ref[:, pl.ds(gate_at + at, FF_TILE)])
        up = mm(nt_ref[...], w_ref[:, pl.ds(gate_at + hidden + at, FF_TILE)])
        back = mm_cols(gres_ref[...], wb_ref[cols, :])
        square = gate * gate
        bend = jnp.tanh(GELU_C * (gate * (1.0 + GELU_A * square)))
        half = 0.5 * (1.0 + bend)
        act = gate * half
        slope = half + (0.5 * GELU_C) * gate * (1.0 - bend * bend) * (1.0 + (3.0 * GELU_A) * square)
        h2_ref[:, cols] = (act * up).astype(BF16)
        gg_ref[:, cols] = (back * up * slope).astype(BF16)
        gu_ref[:, cols] = (back * act).astype(BF16)
        return carry

    lax.fori_loop(0, hidden // FF_TILE, inward, 0)

    def outward(tile, carry):
        cols = pl.ds(pl.multiple_of(tile * QUAD, QUAD), QUAD)
        value = h1_ref[:, cols] + mm(h2_ref[...], wb_ref[:, cols])
        y_ref[:, cols] = (value * valid).astype(BF16)
        gn_ref[:, cols] = mm_cols(gg_ref[...], w_ref[cols, gate_at : gate_at + hidden]) + mm_cols(
            gu_ref[...], w_ref[cols, gate_at + hidden :]
        )
        return carry

    lax.fori_loop(0, D // QUAD, outward, 0)

    def weights(tile, carry):
        at = pl.multiple_of(tile * FF_TILE, FF_TILE)
        cols = pl.ds(at, FF_TILE)
        dg_ref[:, cols] = mm(ntt_ref[...], gg_ref[:, cols]).astype(BF16)
        du_ref[:, cols] = mm(ntt_ref[...], gu_ref[:, cols]).astype(BF16)
        db_ref[cols, :] = mm_rows(h2_ref[:, cols], gres_ref[...]).astype(BF16)
        return carry

    lax.fori_loop(0, hidden // FF_TILE, weights, 0)

    gain_grad = jnp.zeros((1, D), F32)
    for tile in range(TILES):
        rows = pl.ds(tile * QT, QT)
        value, grad = h1_ref[rows, :], gn_ref[rows, :]
        root = lax.rsqrt(mean_square(value) + EPSILON)
        unit = value * root
        gain_grad = gain_grad + jnp.sum(grad * unit, axis=0, keepdims=True)
        grad = grad * gain
        grad = gres_ref[rows, :].astype(F32) + root * (
            grad - unit * jnp.mean(grad * unit, axis=-1, keepdims=True)
        )
        gh_ref[rows, :] = grad
        low = grad.astype(BF16)
        nt_ref[rows, :] = low
        ga_ref[rows, :] = mm_cols(low, w_ref[:, out_at:gate_at]).astype(BF16)

    def out_weight(tile, carry):
        cols = pl.ds(pl.multiple_of(tile * QUAD, QUAD), QUAD)
        do_ref[cols, :] = mm_rows(att_ref[:, cols], nt_ref[...]).astype(BF16)
        return carry

    lax.fori_loop(0, D // QUAD, out_weight, 0)
    return gain_grad


def backward_attention_start(dk_ref, dv_ref):
    dk_ref[...] = jnp.zeros_like(dk_ref)
    dv_ref[...] = jnp.zeros_like(dv_ref)


def backward_attention_quad(tab_ref, rank, qkv_ref, att_ref, ga_ref, lse_ref, dqkv_ref, dk_ref, dv_ref, quad):
    heads = QUAD // DH
    marks = jnp.where(iota((16, QUAD), 1) // DH == iota((16, QUAD), 0), 1.0, 0.0).astype(BF16)
    low = quad * QUAD
    cols = slice(low, low + QUAD)

    def step(tile, carry):
        first = window_start(tile)
        bias, side_bias = tile_bias(tab_ref, rank, tile, first, 0)
        bias = jnp.concatenate([bias, side_bias], axis=0)
        rows = pl.ds(pl.multiple_of(tile * QT, QT), QT)
        window = pl.ds(first, WIN)
        lse = lse_ref[tile]
        product = ga_ref[rows, cols].astype(F32) * att_ref[rows, cols].astype(F32)
        high = product.astype(BF16)
        rest = (product - high.astype(F32)).astype(BF16)
        centre = mm_cols(marks, high) + mm_cols(marks, rest)
        query = head_stack(qkv_ref[rows, cols])
        grad = head_stack(ga_ref[rows, cols])
        keys = jnp.concatenate(
            [qkv_ref[window, D + low : D + low + QUAD], qkv_ref[ROWS:, D + low : D + low + QUAD]], axis=0
        )
        values = jnp.concatenate(
            [qkv_ref[window, 2 * D + low : 2 * D + low + QUAD],
             qkv_ref[ROWS:, 2 * D + low : 2 * D + low + QUAD]], axis=0
        )
        scores = mm_cols(keys, query)
        slopes = mm_cols(values, grad)
        probs, grads = [], []
        for head in range(heads):
            part = slice(head * QT, (head + 1) * QT)
            number = quad * heads + head
            prob = jnp.exp(scores[:, part] + bias - lse[number : number + 1])
            probs.append(prob.astype(BF16))
            grads.append((prob * (slopes[:, part] - centre[head : head + 1])).astype(BF16))
        probs = jnp.concatenate(probs, axis=1)
        grads = jnp.concatenate(grads, axis=1)
        dkey = mm(grads, query)
        dvalue = mm(probs, grad)
        dk_ref[window, cols] = dk_ref[window, cols] + dkey[:WIN]
        dk_ref[ROWS:, cols] = dk_ref[ROWS:, cols] + dkey[WIN:]
        dv_ref[window, cols] = dv_ref[window, cols] + dvalue[:WIN]
        dv_ref[ROWS:, cols] = dv_ref[ROWS:, cols] + dvalue[WIN:]
        dqkv_ref[rows, cols] = head_merge(mm_rows(grads, keys)).astype(BF16)
        return carry

    lax.fori_loop(0, TILES, step, 0)
    dqkv_ref[ROWS:, cols] = jnp.zeros((SIDE_ROWS, QUAD), BF16)
    dqkv_ref[:, D + low : D + low + QUAD] = dk_ref[:, cols].astype(BF16)
    dqkv_ref[:, 2 * D + low : 2 * D + low + QUAD] = dv_ref[:, cols].astype(BF16)


def weight_grads(n_ref, dqkv_ref, refs):
    for number, ref in enumerate(refs):
        def weights(tile, carry):
            at = pl.multiple_of(tile * QUAD, QUAD)
            value = mm_rows(n_ref[...], dqkv_ref[:, pl.ds(number * D + at, QUAD)]).astype(BF16)
            if len(ref.shape) == 4:
                ref[:, :, :, pl.ds(at, QUAD)] = value.reshape(ref.shape[:3] + (QUAD,))
            else:
                ref[:, pl.ds(at, QUAD)] = value
            return carry

        lax.fori_loop(0, D // QUAD, weights, 0)


def backward_project(tab_ref, rank, x_ref, gh_ref, gains, n_ref, dqkv_ref, w_ref, gn_ref, g_ref):
    def step(tile, carry):
        cols = pl.ds(pl.multiple_of(tile * QUAD, QUAD), QUAD)
        gn_ref[:, cols] = mm_cols(dqkv_ref[...], w_ref[cols, : 3 * D])
        return carry

    lax.fori_loop(0, D // QUAD, step, 0)
    pool = pooling(tab_ref, rank)
    side = mm(pool, n_ref[:ROWS, :])
    root = lax.rsqrt(mean_square(side) + EPSILON)
    unit = side * root
    grad = gn_ref[ROWS:, :]
    side_gain = jnp.sum(grad * unit, axis=0, keepdims=True)
    grad = grad * gains[1:2]
    grad = root * (grad - unit * jnp.mean(grad * unit, axis=-1, keepdims=True))
    parts = three_way(grad)
    gain_grad = jnp.zeros((1, D), F32)
    for tile in range(TILES):
        rows = pl.ds(tile * QT, QT)
        spread = pool[:, tile * QT : (tile + 1) * QT]
        total = gn_ref[rows, :] + mm_rows(spread, parts[0]) + mm_rows(spread, parts[1])
        value = x_ref[rows, :].astype(F32)
        root = lax.rsqrt(mean_square(value) + EPSILON)
        unit = value * root
        gain_grad = gain_grad + jnp.sum(total * unit, axis=0, keepdims=True)
        total = total * gains[0:1]
        value = (
            gh_ref[rows, :] + root * (total - unit * jnp.mean(total * unit, axis=-1, keepdims=True))
        ).astype(BF16)
        if len(g_ref.shape) == 3:
            g_ref[pl.ds(tile * (QT // BLK), QT // BLK)] = value.reshape(QT // BLK, BLK, D)
        else:
            g_ref[rows, :] = value
    return gain_grad, side_gain


def first_kernel(tab_ref, x_ref, gc_ref, w_ref, n_ref, qkv_ref, att_ref, lse_ref):
    rank = lax.axis_index("rep")
    gains = gains_of(gc_ref)
    forward_norm(tab_ref, rank, x_ref, gains, n_ref)
    forward_project(n_ref, w_ref, qkv_ref)
    forward_attention(tab_ref, rank, qkv_ref, att_ref, lse_ref, 0, TILES)


def second_kernel(tab_ref, x_ref, cot_ref, att_ref, gc_ref, w_ref, wb_ref,
                  y_ref, gh_ref, ga_ref, dg_ref, du_ref, db_ref, do_ref, gain_ref, *scratch):
    rank = lax.axis_index("rep")
    gain_ref[...] = feed_forward(tab_ref, rank, x_ref, cot_ref, att_ref, gains_of(gc_ref), w_ref, wb_ref,
                                 y_ref, gh_ref, ga_ref, dg_ref, du_ref, db_ref, do_ref, *scratch)


def third_kernel(tab_ref, x_ref, gh_ref, ga_ref, att_ref, lse_ref, n_ref, qkv_ref, gain_ref, gc_ref, w_ref,
                 g_ref, dw_ref, dc_ref, dqkv_ref, dk_ref, dv_ref, gn_ref):
    rank = lax.axis_index("rep")
    gains = gains_of(gc_ref)
    backward_attention_start(dk_ref, dv_ref)
    for quad in range(D // QUAD):
        backward_attention_quad(tab_ref, rank, qkv_ref, att_ref, ga_ref, lse_ref, dqkv_ref, dk_ref, dv_ref, quad)
    weight_grads(n_ref, dqkv_ref, [dw_ref.at[:, i * D : (i + 1) * D] for i in range(3)])
    one, side = backward_project(tab_ref, rank, x_ref, gh_ref, gains, n_ref, dqkv_ref, w_ref, gn_ref, g_ref)
    grads = jnp.concatenate([one, side, gain_ref[...], jnp.zeros((5, D), F32)], axis=0)
    spread_gain_grads(grads, dc_ref)


def attend(tab, x, gc, w):
    shape = jax.ShapeDtypeStruct
    return pl.pallas_call(
        first_kernel,
        out_shape=(shape((ALL_ROWS, D), BF16), shape((ALL_ROWS, 3 * D), BF16), shape((ROWS, D), BF16),
                   shape((TILES, 16, QT), F32)),
        in_specs=[SMEM, VMEM, VMEM, pl.BlockSpec((D, 3 * D), lambda step: (0, 0))],
        grid=(1,),
        out_specs=(VMEM,) * 4,
        compiler_params=pltpu.CompilerParams(vmem_limit_bytes=VMEM_LIMIT),
        name="attend",
    )(tab, x, gc, w)


def feed(tab, x, cot, att, gc, w, wb):
    hidden = wb.shape[0]
    shape = jax.ShapeDtypeStruct
    return pl.pallas_call(
        second_kernel,
        out_shape=(shape((ROWS, D), BF16), shape((ROWS, D), F32), shape((ROWS, D), BF16),
                   shape((D, hidden), BF16), shape((D, hidden), BF16), shape((hidden, D), BF16), shape((D, D), BF16),
                   shape((1, D), F32)),
        in_specs=[SMEM] + [VMEM] * 6,
        out_specs=(VMEM,) * 8,
        scratch_shapes=[pltpu.VMEM((ROWS, D), F32), pltpu.VMEM((ROWS, D), BF16), pltpu.VMEM((D, ROWS), BF16),
                        pltpu.VMEM((ROWS, D), BF16), pltpu.VMEM((ROWS, hidden), BF16),
                        pltpu.VMEM((ROWS, hidden), BF16), pltpu.VMEM((ROWS, hidden), BF16),
                        pltpu.VMEM((ROWS, D), F32)],
        compiler_params=pltpu.CompilerParams(vmem_limit_bytes=VMEM_LIMIT),
        name="feed_forward",
    )(tab, x, cot, att, gc, w, wb)


def backward_layer(tab, x, gh, ga, att, lse, n, qkv, gain, gc, w):
    shape = jax.ShapeDtypeStruct
    return pl.pallas_call(
        third_kernel,
        out_shape=(shape((ROWS, D), BF16), shape((D, 3 * D), BF16), shape((gc.shape[0], 8, 128), F32)),
        in_specs=[SMEM] + [VMEM] * 9 + [pl.BlockSpec((D, 3 * D), lambda step: (0, 0))],
        grid=(1,),
        out_specs=(VMEM,) * 3,
        scratch_shapes=[pltpu.VMEM((ALL_ROWS, 3 * D), BF16), pltpu.VMEM((ALL_ROWS, D), F32),
                        pltpu.VMEM((ALL_ROWS, D), F32), pltpu.VMEM((ALL_ROWS, D), F32)],
        compiler_params=pltpu.CompilerParams(vmem_limit_bytes=VMEM_LIMIT),
        name="attend_back",
    )(tab, x, gh, ga, att, lse, n, qkv, gain, gc, w)


class Links:
    def __init__(self, outer, inner):
        self.outer, self.inner = outer, inner
        self.rank, self.spot = lax.axis_index("rep"), lax.axis_index("fsdp")
        self.core = self.rank % 2
        self.row, self.col = self.spot // inner, self.spot % inner
        self.mate, self.across = core_of(self.rank), across_of(self.rank)
        self.late = []

    def greet(self, everyone=False):
        barrier = pltpu.get_barrier_semaphore()
        neighbours = (
            (self.row + 1 < self.outer, {"fsdp": self.spot + self.inner}),
            (self.row > 0, {"fsdp": self.spot - self.inner}),
            (self.col + 1 < self.inner, {"fsdp": self.spot + 1}),
            (self.col > 0, {"fsdp": self.spot - 1}),
        )
        group = (self.mate, self.across) + ((across_of(self.mate),) if everyone else ())
        amount = jnp.int32(len(group))
        for there, device in neighbours:
            amount = amount + there.astype(jnp.int32)

            @pl.when(there)
            def _():
                pl.semaphore_signal(barrier, inc=1, device_id=device, device_id_type=MESH)

        for device in group:
            pl.semaphore_signal(barrier, inc=1, device_id={"rep": device}, device_id_type=MESH)
        pl.semaphore_wait(barrier, amount)

    def send(self, there, src, dst, ssem, rsem, device):
        def describe():
            return pltpu.make_async_remote_copy(
                src_ref=src, dst_ref=dst, send_sem=ssem, recv_sem=rsem,
                device_id=device, device_id_type=MESH,
            )

        if there is None:
            describe().start()
        else:
            @pl.when(there)
            def _():
                describe().start()

        self.late.append((there, lambda: describe().wait_send()))

    def arrive(self, place, rsem, spare):
        pltpu.make_async_remote_copy(
            src_ref=place, dst_ref=place, send_sem=spare, recv_sem=rsem,
            device_id={"rep": self.mate}, device_id_type=MESH,
        ).wait_recv()

    def drain(self):
        for there, finish in self.late:
            if there is None:
                finish()
            else:
                pl.when(there)(finish)


def halves(ref, which):
    half = ref.shape[-1] // 2
    cols = pl.ds(pl.multiple_of(which * half, 128), half)
    return ref.at[:, :, :, cols] if len(ref.shape) == 4 else ref.at[:, cols]


class Reduction:
    def __init__(self, links, source, total, mine, crecv, yrecv, zrecv, xrecv, stage, sems, number):
        self.links, self.source, self.total, self.mine, self.stage = links, source, total, mine, stage
        self.crecv, self.yrecv, self.zrecv, self.xrecv = crecv, yrecv, zrecv, xrecv
        self.sems, self.number = sems, number
        self.whole = total.shape[-1] % 256 != 0
        self.load = None

    def sem(self, name, *index):
        return self.sems[name].at[index + (self.number,)]

    def begin(self):
        links = self.links
        other = self.source if self.whole else halves(self.source, 1 - links.core)
        links.send(None, other, self.crecv, self.sem("c_send"), self.sem("c_recv"), {"rep": links.mate})
        if self.mine is None:
            self.mine = self.source if self.whole else halves(self.source, links.core)
        else:
            own = self.source if self.whole else halves(self.source, links.core)
            self.load = pltpu.make_async_copy(own, self.mine, self.sem("m_sem"))
            self.load.start()

    def pair(self):
        links = self.links
        if self.load is not None:
            self.load.wait()
        links.arrive(self.crecv, self.sem("c_recv"), self.sems["spare"].at[0])
        inner = links.inner

        def add(index, carry):
            row, col = index // inner, index % inner
            self.mine[row, col] = self.mine[row, col] + self.crecv[row, col]
            return carry

        lax.fori_loop(0, links.outer * inner, add, 0)
        links.send(None, self.mine.at[:, 1 - links.col], self.yrecv, self.sem("y_send"), self.sem("y_recv"),
                   {"fsdp": links.spot + 1 - 2 * links.col})

    def slot(self, way, place, dest):
        return dest - place if way == 0 else self.links.outer - place + dest

    def pass_on(self, way, dest, there, first):
        links = self.links
        step = 1 if way == 0 else -1
        mine = self.mine.at[dest, links.col]
        put = self.slot(way, links.row + step, dest)
        if not first:
            got = self.slot(way, links.row, dest)

            @pl.when(there)
            def _():
                links.arrive(self.zrecv.at[got], self.sem("z_recv", got), self.sems["spare"].at[0])
                mine[...] = mine[...] + self.zrecv[got]

        links.send(there, mine, self.zrecv.at[put], self.sem("z_send", way, dest), self.sem("z_recv", put),
                   {"fsdp": links.spot + step * links.inner})

    def column(self):
        links = self.links
        size = links.outer
        links.arrive(self.yrecv, self.sem("y_recv"), self.sems["spare"].at[0])

        def add(index, carry):
            self.mine[index, links.col] = self.mine[index, links.col] + self.yrecv[index]
            return carry

        lax.fori_loop(0, size, add, 0)
        for far in range(size - 1, 0, -1):
            self.pass_on(0, far, links.row == 0, True)
            self.pass_on(1, size - 1 - far, links.row == size - 1, True)

    def hop(self, turn):
        links = self.links
        size = links.outer
        for way in range(2):
            place = turn if way == 0 else size - 1 - turn
            here = links.row == place
            rest = range(size - 1, place, -1) if way == 0 else range(0, place)
            for dest in rest:
                self.pass_on(way, dest, here, False)
            mine = self.mine.at[place, links.col]
            got = self.slot(way, place, place)

            @pl.when(here)
            def _():
                links.arrive(self.zrecv.at[got], self.sem("z_recv", got), self.sems["spare"].at[0])
                mine[...] = mine[...] + self.zrecv[got]

    def cross(self):
        links = self.links
        mine = self.mine.at[links.row, links.col]
        links.send(None, mine, self.xrecv, self.sem("x_send"), self.sem("x_recv"), {"rep": links.across})

    def finish(self):
        links = self.links
        links.arrive(self.xrecv, self.sem("x_recv"), self.sems["spare"].at[0])
        self.stage[...] = self.mine[links.row, links.col].astype(F32) + self.xrecv[...].astype(F32)
        place = self.total if self.whole else halves(self.total, links.core)
        self.keep = pltpu.make_async_copy(self.stage, place, self.sem("m_sem"))
        self.keep.start()
        if not self.whole:
            links.send(None, self.stage, place, self.sem("f_send"), self.sem("f_recv"), {"rep": links.mate})

    def settle(self):
        self.keep.wait()
        if not self.whole:
            self.links.arrive(
                halves(self.total, 1 - self.links.core), self.sem("f_recv"), self.sems["spare"].at[0]
            )


class AcrossFirst(Reduction):
    def pair(self):
        links = self.links
        if self.load is not None:
            self.load.wait()
        links.arrive(self.crecv, self.sem("c_recv"), self.sems["spare"].at[0])
        inner = links.inner

        def add(index, carry):
            row, col = index // inner, index % inner
            self.mine[row, col] = self.mine[row, col] + self.crecv[row, col]
            return carry

        lax.fori_loop(0, links.outer * inner, add, 0)
        self.side = links.rank // 2
        links.send(None, self.rows_of(self.mine, 1 - self.side), self.xrecv, self.sem("x_send"), self.sem("x_recv"),
                   {"rep": links.across})

    def rows_of(self, ref, which):
        half = ref.shape[-2] // 2
        rows = pl.ds(pl.multiple_of(which * half, 16), half)
        return ref.at[:, :, rows, :] if len(ref.shape) == 4 else ref.at[rows, :]

    def meet(self):
        links = self.links
        links.arrive(self.xrecv, self.sem("x_recv"), self.sems["spare"].at[0])
        self.mine = self.rows_of(self.mine, self.side)
        inner = links.inner

        def add(index, carry):
            row, col = index // inner, index % inner
            self.mine[row, col] = self.mine[row, col] + self.xrecv[row, col]
            return carry

        lax.fori_loop(0, links.outer * inner, add, 0)
        links.send(None, self.mine.at[:, 1 - links.col], self.yrecv, self.sem("y_send"), self.sem("y_recv"),
                   {"fsdp": links.spot + 1 - 2 * links.col})

    def quarter(self, side, core):
        return halves(self.rows_of(self.total, side), core)

    def spread(self, stage, place, keep, ssem, rsem):
        links = self.links
        self.keeps.append(pltpu.make_async_copy(stage, place, keep))
        self.keeps[-1].start()
        links.send(None, stage, place, ssem, rsem, {"rep": links.mate})

    def cross(self):
        links = self.links
        mine = self.mine.at[links.row, links.col]
        links.send(None, mine, self.third, self.sem("h_send"), self.sem("h_recv"), {"rep": links.across})
        self.stage[...] = mine[...].astype(F32)
        self.keeps = []
        self.spread(self.stage, self.quarter(self.side, links.core), self.sem("m_sem"),
                    self.sem("f_send"), self.sem("f_recv"))

    def finish(self):
        links = self.links
        links.arrive(self.third, self.sem("h_recv"), self.sems["spare"].at[0])
        self.stage_two[...] = self.third[...].astype(F32)
        self.spread(self.stage_two, self.quarter(1 - self.side, links.core), self.sem("k_keep"),
                    self.sem("k_send"), self.sem("k_recv"))

    def settle(self):
        links = self.links
        for keep in self.keeps:
            keep.wait()
        for side, name in ((self.side, "f_recv"), (1 - self.side, "k_recv")):
            links.arrive(self.quarter(side, 1 - links.core), self.sem(name), self.sems["spare"].at[0])


SEM_NAMES = ("c_send", "c_recv", "m_sem", "y_send", "y_recv", "z_send", "z_recv", "x_send", "x_recv",
             "f_send", "f_recv", "h_send", "h_recv", "k_send", "k_recv", "k_keep", "r_send", "r_recv", "own", "spare")


class Return:
    def __init__(self, links, source, home, sems, kind):
        self.links, self.source, self.home, self.sems, self.kind = links, source, home, sems, kind

    def begin(self):
        links = self.links
        dst = self.home.at[links.rank]
        for way, device in enumerate((links.across, links.mate)):
            links.send(None, self.source, dst, self.sems["r_send"].at[self.kind, way],
                       self.sems["r_recv"].at[self.kind, way], {"rep": device})
        self.copy = pltpu.make_async_copy(self.source, dst, self.sems["own"].at[self.kind])
        self.copy.start()

    def relay(self):
        links = self.links
        place = self.home.at[links.across]
        links.arrive(place, self.sems["r_recv"].at[self.kind, 0], self.sems["spare"].at[0])
        links.send(None, place, place, self.sems["r_send"].at[self.kind, 2],
                   self.sems["r_recv"].at[self.kind, 2], {"rep": links.mate})

    def settle(self):
        links, sem = self.links, self.sems["r_recv"]
        links.arrive(self.home.at[links.mate], sem.at[self.kind, 1], self.sems["spare"].at[0])
        links.arrive(self.home.at[across_of(links.mate)], sem.at[self.kind, 2], self.sems["spare"].at[0])
        self.copy.wait()


TABLE_ROWS = 56


def packed_table(lens, tabv_ref):
    lane = iota((8, 128), 1)
    blocks = lax.div(lens + (BLK - 1), BLK)
    key = jnp.where(blocks > 0, blocks * 128 + (127 - lane), 0)
    wide = jnp.broadcast_to(key[:1], (128, 128))
    other = jnp.sum(jnp.where(iota((128, 128), 0) == iota((128, 128), 1), wide, 0), axis=1, keepdims=True)
    order = jnp.sum(jnp.where(other > wide, 1, 0), axis=0, keepdims=True)
    order = jnp.broadcast_to(order, (8, 128))
    edges, below = [], jnp.zeros((8, 1), jnp.int32)
    for size in range(MAX_SEQ_BLOCKS, 0, -1):
        below = below + jnp.sum(jnp.where(blocks == size, 1, 0), axis=1, keepdims=True)
        edges.append(jnp.broadcast_to(below, (8, 128)))

    def assign(number, carry):
        loads, slot, first = carry[:4], carry[4], carry[5]
        size = jnp.zeros((8, 128), jnp.int32)
        for step, edge in enumerate(edges):
            size = size + jnp.where(number < edge, 1, 0)
        low = jnp.minimum(jnp.minimum(loads[0], loads[1]), jnp.minimum(loads[2], loads[3]))
        best = jnp.full((8, 128), 3, jnp.int32)
        for dev in (2, 1, 0):
            best = jnp.where(loads[dev] == low, dev, best)
        mine = order == number
        slot = jnp.where(mine, best * SLOTS + low, slot)
        first = jnp.where(mine, low, first)
        loads = tuple(loads[dev] + jnp.where(best == dev, size, 0) for dev in range(4))
        return loads + (slot, first)

    zero = jnp.zeros((8, 128), jnp.int32)
    carry = lax.fori_loop(0, 32, assign, (zero,) * 6)
    slot, first = carry[4], carry[5]
    where, tokens, segment = zero - 1, zero, zero
    for step in range(MAX_SEQ_BLOCKS):
        def shifted(value):
            return value if step == 0 else pltpu.roll(value, step, 1)

        covers = shifted(blocks) > step
        where = jnp.where(covers, shifted(slot) + step, where)
        tokens = jnp.where(covers, jnp.minimum(shifted(lens) - BLK * step, BLK), tokens)
        segment = jnp.where(covers, shifted(first) + 1, segment)
    packed = jnp.where(where >= 0, (lane + 1) + 128 * tokens + 16384 * segment, 0)
    spots = jnp.broadcast_to(where[:1], (48, 128))
    values = jnp.broadcast_to(packed[:1], (48, 128))
    column = jnp.sum(jnp.where(spots == iota((48, 128), 0), values, 0), axis=1, keepdims=True)
    tabv_ref[:48] = jnp.broadcast_to(column, (48, 128))
    tabv_ref[48:] = where


FRONT_ORDER = (
    ("own", 5), ("own", 0), ("own", 1), ("own", 2), ("do", "table"), ("hop", 5, 0), ("pack", 0, 1), ("pack", 1, 1),
    ("cross", 0), ("pack", 0, 0), ("hop", 0, 0), ("hop", 5, 1), ("cross", 1), ("pack", 1, 0), ("hop", 1, 0),
    ("hop", 2, 0), ("hop", 0, 1), ("hop", 5, 2), ("hop", 1, 1), ("own", 3), ("hop", 2, 1), ("own", 4), ("hop", 0, 2),
    ("hop", 1, 2), ("hop", 3, 0), ("fr", 5), ("rfin", 0), ("do", "norm"), ("hop", 2, 2), ("hop", 4, 0),
    ("hop", 3, 1), ("fr", 0), ("hop", 4, 1), ("got", 0), ("do", "proj"), ("hop", 3, 2), ("fr", 1), ("do", "a0"),
    ("hop", 4, 2), ("fr", 2), ("do", "a1"), ("rfin", 1), ("do", "a2"), ("fr", 3), ("xin", 1), ("fr", 4), ("got", 1),
    ("got", 2), ("got", 3), ("got", 4),
)


def front_kernel(outer, inner, *refs):
    (lens_ref, rows_any, cots_any, *weights), refs = refs[:9], refs[9:]
    (wd_ref, wc_ref), refs = refs[:2], refs[2:]
    tab_ref, outs_any, (ga_ref, gb_ref), refs = refs[0], refs[1:9], refs[9:11], refs[11:]
    (stage, lens_all, tabs, psend, precv, xsend, xrecv, rows_ref, cots_ref), refs = refs[:9], refs[9:]
    held, refs = refs[:8], refs[8:]
    x_ref, cot_ref, n_ref, qkv_ref, att_ref, lse_ref, wqkv_ref, gc_ref = held
    (l_send, l_recv, t_sem, w_sem, z_send, z_recv, y_send, y_recv, c_send, c_recv, d_send, d_recv, own_sem,
     p_send, p_recv, x_send, x_recv, spare, out_sem) = refs
    links = Links(outer, inner)
    rank, spot, core, mate, across = links.rank, links.spot, links.core, links.mate, links.across
    row, col = links.row, links.col
    side = rank // 2
    count = outer * inner
    part = stage.shape[0]
    per_rank = rows_ref.shape[0]
    width = 3 * D
    tall = wd_ref.shape[0]
    hidden = weights[-1].shape[1]
    rest = stage.shape[1] - width
    cuts = [0, 7 * rest // 19, 13 * rest // 19, rest]
    spans = [(cuts[i], (cuts[i + 1] - cuts[i]) // 2) for i in range(3)]

    at = 0
    loads = []
    row_loads = [pltpu.make_async_copy(rows_any, rows_ref, w_sem.at[6]), pltpu.make_async_copy(cots_any, cots_ref, w_sem.at[7])]
    for number, ref in enumerate(weights):
        cols = slice(at, at + ref.shape[1])
        loads.append(pltpu.make_async_copy(ref, stage.at[:, cols], w_sem.at[number]))
        loads[-1].start()
        at += ref.shape[1]
    for load in row_loads:
        load.start()

    links.greet(True)
    lens_all[rank] = lens_ref[...]
    for step in range(1, 4):
        links.send(None, lens_ref, lens_all.at[rank], l_send.at[step - 1], l_recv.at[step - 1],
                   {"rep": (rank + step) % 4})

    def cols_of(start, half, which):
        return pl.ds(pl.multiple_of(start + which * half, 128), half)

    down_half = D // 2

    def tall_rows(which):
        return pl.ds(pl.multiple_of(which * (tall // 2), 16), tall // 2)

    def source(number):
        if number == 0:
            return stage.at[:, cols_of(0, width // 2, core)]
        if number == 1:
            return wd_ref.at[tall_rows(side), cols_of(0, down_half, core)]
        if number == 5:
            return wc_ref
        start, half = spans[number - 2]
        return stage.at[:, cols_of(width + start, half, core)]

    def place(number, shard, which=None):
        which = core if which is None else which
        if number == 0:
            return wqkv_ref.at[pl.ds(pl.multiple_of(shard * part, 16), part), cols_of(0, width // 2, which)]
        if number in (1, 6):
            return gb_ref.at[shard, tall_rows(side if number == 1 else 1 - side), cols_of(0, down_half, which)]
        if number == 5:
            return gc_ref.at[shard]
        start, half = spans[number - 2]
        return ga_ref.at[shard, :, cols_of(start, half, which)]

    nobody = spare.at[0]

    def both(first, second):
        return second if first is None else jnp.logical_and(first, second)

    def guarded(there, action):
        if there is None:
            action()
        else:
            pl.when(there)(action)

    def share(there, number, shard):
        if number == 5:
            return
        here = place(number, shard)
        links.send(there, here, here, c_send.at[number, shard], c_recv.at[number, shard], {"rep": mate})
        if number == 1:
            links.send(there, here, here, d_send.at[shard], d_recv.at[shard], {"rep": across})

    other_column = {"fsdp": spot + 1 - 2 * col}

    def along_row(there, number, line, src):
        here = place(number, line * inner + col)
        links.send(there, here if src is None else src, here, y_send.at[line, number], y_recv.at[line, number],
                   other_column)

    def lines(step):
        return ((row - 1 - step >= 0, row - 1 - step, 0, row + 1 < outer, spot + inner),
                (row + 1 + step < outer, row + 1 + step, 1, row > 0, spot - inner))

    def own(number):
        src, dst = source(number), place(number, spot)
        links.send(row + 1 < outer, src, dst, z_send.at[0, 0, number], z_recv.at[0, 0, number],
                   {"fsdp": spot + inner})
        links.send(row > 0, src, dst, z_send.at[1, 0, number], z_recv.at[1, 0, number], {"fsdp": spot - inner})
        along_row(None, number, row, src)

    def hop(number, step):
        for here, line, way, onward, target in lines(step):
            shard = line * inner + col
            guarded(here, lambda: links.arrive(place(number, shard), z_recv.at[way, step, number], nobody))
            if step + 1 < outer - 1:
                view = place(number, shard)
                links.send(both(here, onward), view, view, z_send.at[way, step + 1, number],
                           z_recv.at[way, step + 1, number], {"fsdp": target})
            along_row(here, number, line, None)
            share(here, number, shard)

    def from_row(number):
        def one(there, line):
            shard = line * inner + 1 - col
            guarded(there, lambda: links.arrive(place(number, shard), y_recv.at[line, number], nobody))
            share(there, number, shard)

        one(None, row)
        for step in range(outer - 1):
            for here, line, *_ in lines(step):
                one(here, line)

    def gathered(*numbers):
        def wait(shard, carry):
            @pl.when(shard != spot)
            def _():
                for number in numbers:
                    links.arrive(place(number, shard, 1 - core), c_recv.at[number, shard], nobody)

            return carry

        lax.fori_loop(0, count, wait, 0)

    def from_across():
        def relay(shard, carry):
            here = place(6, shard)

            @pl.when(shard != spot)
            def _():
                links.arrive(here, d_recv.at[shard], nobody)
                pltpu.make_async_remote_copy(
                    src_ref=here, dst_ref=here, send_sem=c_send.at[6, shard], recv_sem=c_recv.at[6, shard],
                    device_id={"rep": mate}, device_id_type=MESH,
                ).start()

            return carry

        lax.fori_loop(0, count, relay, 0)

    for load in loads:
        load.wait()
    keep = [
        pltpu.make_async_copy(stage.at[:, :width], wqkv_ref.at[pl.ds(pl.multiple_of(spot * part, 16), part)], own_sem.at[0]),
        pltpu.make_async_copy(stage.at[:, width:], ga_ref.at[spot], own_sem.at[1]),
        pltpu.make_async_copy(wd_ref, gb_ref.at[spot], own_sem.at[2]),
        pltpu.make_async_copy(wc_ref, gc_ref.at[spot], own_sem.at[3]),
    ]
    for copy in keep:
        copy.start()
    leaving = []

    def leave(*numbers):
        for number in numbers:
            leaving.append(pltpu.make_async_copy(held[number], outs_any[number], out_sem.at[number]))
            leaving[-1].start()

    def make_table():
        for step in range(1, 4):
            links.arrive(lens_all.at[(rank + 4 - step) % 4], l_recv.at[step - 1], nobody)
        lens = lens_all[0] + lens_all[1] + lens_all[2] + lens_all[3]
        packed_table(jnp.broadcast_to(lens[:1], (8, 128)), tab_ref)
        to_scalar = pltpu.make_async_copy(tab_ref, tabs, t_sem.at[0])
        to_scalar.start()
        to_scalar.wait()
        for load in row_loads:
            load.wait()

    sources = (rows_ref, cots_ref)
    outs = (x_ref, cot_ref)

    def picked(kind, target, slot):
        index = block_at(tabs, target * SLOTS + slot) - rank * per_rank
        mine = jnp.logical_and(index >= 0, index < per_rank)
        return mine, sources[kind][jnp.clip(index, 0, per_rank - 1)]

    def mate_copy(kind, piece):
        return pltpu.make_async_remote_copy(
            src_ref=psend.at[kind, piece], dst_ref=precv.at[kind, piece],
            send_sem=p_send.at[kind, piece], recv_sem=p_recv.at[kind, piece],
            device_id={"rep": mate}, device_id_type=MESH,
        )

    def across_copy(kind):
        return pltpu.make_async_remote_copy(
            src_ref=xsend.at[kind], dst_ref=xrecv.at[kind],
            send_sem=x_send.at[kind], recv_sem=x_recv.at[kind],
            device_id={"rep": across}, device_id_type=MESH,
        )

    def pack_rows(kind, piece):
        target = mate if piece == 0 else across_of(mate)

        def pack(slot, carry):
            mine, value = picked(kind, target, slot)
            psend[kind, piece, slot] = jnp.where(mine, value, jnp.zeros_like(value))
            return carry

        lax.fori_loop(0, SLOTS, pack, 0)
        mate_copy(kind, piece).start()

    def cross_rows(kind):
        mate_copy(kind, 1).wait_recv()

        def merge(slot, carry):
            mine, value = picked(kind, across, slot)
            xsend[kind, slot] = jnp.where(mine, value, precv[kind, 1, slot])
            return carry

        lax.fori_loop(0, SLOTS, merge, 0)
        across_copy(kind).start()

    def finish_rows(kind):
        mate_copy(kind, 0).wait_recv()
        across_copy(kind).wait_recv()

        def finish(slot, carry):
            mine, value = picked(kind, rank, slot)
            rows = pl.ds(pl.multiple_of(slot * BLK, BLK), BLK)
            outs[kind][rows, :] = jnp.where(mine, value, precv[kind, 0, slot] + xrecv[kind, slot])
            return carry

        lax.fori_loop(0, SLOTS, finish, 0)

    def norm():
        keep[3].wait()
        forward_norm(tabs, rank, x_ref, gains_of(gc_ref), n_ref)
        leave(2, 7)

    def project():
        keep[0].wait()
        forward_project(n_ref, wqkv_ref, qkv_ref)
        leave(3, 6)

    def attend_tiles(begin, end):
        forward_attention(tabs, rank, qkv_ref, att_ref, lse_ref, begin, end)
        if end == TILES:
            leave(4, 5)

    work = {"table": make_table, "norm": norm, "proj": project, "a0": lambda: attend_tiles(0, 2),
            "a1": lambda: attend_tiles(2, 4), "a2": lambda: attend_tiles(4, TILES)}
    tail = []
    for action, which, *more in FRONT_ORDER:
        if action == "do":
            work[which]()
        elif action == "own":
            own(which)
        elif action == "hop":
            hop(which, more[0])
        elif action == "fr":
            from_row(which)
        elif action == "xin":
            from_across()
        elif action == "got" and which == 0:
            gathered(0)
        elif action == "got":
            tail.append(which)
        elif action == "pack":
            pack_rows(which, more[0])
        elif action == "cross":
            cross_rows(which)
        else:
            finish_rows(which)
            leave(which)
    gathered(*tail, 6)

    def sent(shard, carry):
        @pl.when(shard != spot)
        def _():
            pltpu.make_async_remote_copy(
                src_ref=place(6, shard), dst_ref=place(6, shard), send_sem=c_send.at[6, shard], recv_sem=c_recv.at[6, shard],
                device_id={"rep": mate}, device_id_type=MESH,
            ).wait_send()

        return carry

    lax.fori_loop(0, count, sent, 0)
    links.drain()
    for kind in range(2):
        for piece in range(2):
            mate_copy(kind, piece).wait_send()
        across_copy(kind).wait_send()
    for copy in keep[1:3] + leaving:
        copy.wait()


def gather_and_attend(count, lens, rows, cots, weights, wd, wc):
    outer, inner = grid_of(count)
    block = rows.shape[1:]
    part, hidden = wd.shape[0], weights[-1].shape[1]
    part = weights[0].shape[0]
    dma, shape = pltpu.SemaphoreType.DMA, jax.ShapeDtypeStruct
    total = sum(weight.shape[1] for weight in weights)
    kinds = 6
    held = (shape((ROWS, D), BF16), shape((ROWS, D), BF16), shape((ALL_ROWS, D), BF16), shape((ALL_ROWS, 3 * D), BF16),
            shape((ROWS, D), BF16), shape((TILES, 16, QT), F32), shape((D, 3 * D), BF16), shape((count,) + wc.shape, BF16))
    return pl.pallas_call(
        partial(front_kernel, outer, inner),
        out_shape=(shape((TABLE_ROWS, 128), jnp.int32),) + held + (
            shape((count, part, total - 3 * D), BF16), shape((count,) + wd.shape, BF16),
        ),
        in_specs=[VMEM] + [ANY] * 8 + [VMEM] * 2,
        out_specs=(VMEM,) + (ANY,) * 10,
        scratch_shapes=[
            pltpu.VMEM((part, total), BF16), pltpu.VMEM((4, 8, 128), jnp.int32), pltpu.SMEM((TABLE_ROWS, 128), jnp.int32),
            pltpu.VMEM((2, 2, SLOTS) + block, BF16), pltpu.VMEM((2, 2, SLOTS) + block, BF16),
            pltpu.VMEM((2, SLOTS) + block, BF16), pltpu.VMEM((2, SLOTS) + block, BF16),
            pltpu.VMEM(rows.shape, BF16), pltpu.VMEM(cots.shape, BF16),
            *(pltpu.VMEM(one.shape, one.dtype) for one in held),
            dma((3,)), dma((3,)), dma((1,)), dma((8,)),
            dma((2, outer - 1, kinds)), dma((2, outer - 1, kinds)), dma((outer, kinds)), dma((outer, kinds)),
            dma((kinds + 1, count)), dma((kinds + 1, count)), dma((count,)), dma((count,)), dma((4,)),
            dma((2, 2)), dma((2, 2)), dma((2,)), dma((2,)), dma((1,)), dma((8,)),
        ],
        compiler_params=pltpu.CompilerParams(
            collective_id=1, has_side_effects=True, vmem_limit_bytes=VMEM_LIMIT
        ),
        name="gather_and_attend",
    )(lens, rows, cots, *weights, wd, wc)


ACROSS_FIRST = (2, 3)
REAR_ORDER = (
    ("do", "start"), ("do", "P0"), ("do", "P1a"), ("do", "gA"), ("begin", 0), ("do", "uA"), ("begin", 1),
    ("do", "P1b"), ("pair", 0), ("pair", 1), ("do", "gB"), ("begin", 2), ("do", "uB"), ("begin", 3), ("do", "d"),
    ("begin", 4), ("pair", 2), ("pair", 3), ("do", "out"), ("rows", 0), ("pair", 4), ("col", 0), ("meet", 2),
    ("do", "P4"), ("col", 1), ("do", "P5"), ("begin", 5), ("do", "q0"), ("meet", 3), ("pair", 5), ("hop", 0, 1),
    ("hop", 1, 1), ("do", "p0"), ("begin", 6), ("do", "q1"), ("pair", 6), ("col", 4), ("hop", 0, 2), ("hop", 1, 2),
    ("do", "p1"), ("begin", 7), ("do", "q2"), ("pair", 7), ("col", 2), ("col", 3), ("hop", 0, 3), ("cross", 0),
    ("hop", 1, 3), ("cross", 1), ("do", "bp"), ("rows", 1), ("relay", 0), ("col", 5), ("hop", 4, 1), ("fin", 0),
    ("fin", 1), ("do", "p2"), ("begin", 8), ("hop", 2, 1), ("do", "dc"), ("begin", 9), ("hop", 3, 1), ("pair", 8),
    ("pair", 9), ("col", 6), ("hop", 4, 2), ("hop", 5, 1), ("hop", 2, 2), ("hop", 3, 2), ("hop", 6, 1),
    ("hop", 5, 2), ("hop", 6, 2), ("hop", 4, 3), ("cross", 4), ("col", 7), ("hop", 7, 1), ("hop", 2, 3),
    ("cross", 2), ("hop", 3, 3), ("cross", 3), ("col", 8), ("col", 9), ("hop", 5, 3), ("cross", 5), ("hop", 6, 3),
    ("cross", 6), ("relay", 1), ("hop", 8, 1), ("hop", 9, 1), ("hop", 7, 2), ("hop", 8, 2), ("hop", 9, 2),
    ("fin", 4), ("fin", 2), ("fin", 3), ("hop", 7, 3), ("cross", 7), ("fin", 5), ("hop", 8, 3), ("cross", 8),
    ("hop", 9, 3), ("cross", 9), ("fin", 6), ("fin", 7), ("fin", 8), ("fin", 9),
)


def rear_kernel(outer, inner, *refs):
    (tab_ref, x_ref, att_ref, lse_ref, gc_ref), refs = refs[:5], refs[5:]
    (cot_any, n_any, qkv_any, wqkv_any, wf_any, wd_any), refs = refs[:6], refs[6:]
    kinds = 10
    (og_ref, ou_ref, od_ref, oo_ref, op_ref, oc_ref, ry_ref, rg_ref), refs = refs[:8], refs[8:]
    (y_ref, gh_ref, fa_ref, dk_ref, b0_ref, b1_ref, b2_ref, n_ref, ntt_ref, gres_ref, ga_ref), refs = refs[:11], refs[11:]
    (wf_ref, wd_ref, dg_ref, du_ref, db_ref, do_ref, dc_ref, mine_ref), refs = refs[:8], refs[8:]
    crecv, refs = list(refs[:7]), refs[7:]
    narrow = D // 2
    crecv = crecv[:6] + [crecv[i].at[:, :, :, :narrow] for i in range(3)] + crecv[6:]
    yrecv, zrecv, xrecv, stages = (refs[kinds * i : kinds * (i + 1)] for i in range(4))
    refs = refs[4 * kinds :]
    extra, refs = refs[: 2 * len(ACROSS_FIRST)], refs[2 * len(ACROSS_FIRST) :]
    sems = dict(zip(SEM_NAMES, refs))
    load_sem, free_sem = refs[len(SEM_NAMES) :]
    links = Links(outer, inner)
    rank = links.rank
    hidden = wd_ref.shape[0]
    part = wf_ref.shape[2]
    group = 4 * part

    def fetch(number, src, dst):
        copy = pltpu.make_async_copy(src, dst, load_sem.at[number])
        copy.start()
        return copy

    load_cot = fetch(0, cot_any, ga_ref)
    load_out = fetch(1, wf_any.at[:, :, :, :D], wf_ref.at[:, :, :, :D])
    load_in = fetch(2, wf_any.at[:, :, :, D:], wf_ref.at[:, :, :, D:])
    load_down = fetch(3, wd_any, wd_ref)
    links.greet()

    def weight(start, size):
        return wf_ref[:, :, :, pl.ds(start, size)].reshape(D, size)

    wide = hidden // 2
    first, second = slice(0, wide), slice(wide, hidden)
    grads = [dg_ref.at[:, :, :, first], du_ref.at[:, :, :, first], dg_ref.at[:, :, :, second], du_ref.at[:, :, :, second],
             db_ref, do_ref] + [wf_ref.at[:, :, :, i * D : (i + 1) * D] for i in range(3)] + [dc_ref]
    totals = [og_ref.at[:, first], ou_ref.at[:, first], og_ref.at[:, second], ou_ref.at[:, second],
              od_ref, oo_ref] + [op_ref.at[:, i * D : (i + 1) * D] for i in range(3)] + [oc_ref]
    tasks = [
        (AcrossFirst if i in ACROSS_FIRST else Reduction)(
            links, grads[i], totals[i], mine_ref if i == kinds - 1 else None,
            crecv[i], yrecv[i], zrecv[i], xrecv[i], stages[i], sems, i,
        )
        for i in range(kinds)
    ]
    for number, i in enumerate(ACROSS_FIRST):
        tasks[i].third, tasks[i].stage_two = extra[2 * number], extra[2 * number + 1]
    returns = (Return(links, y_ref, ry_ref, sems, 0), Return(links, gres_ref, rg_ref, sems, 1))
    gains = gains_of(gc_ref)
    gain = gains[2:3]
    valid = valid_column(tab_ref, rank)
    h1_ref, dv_ref = fa_ref, fa_ref
    tiles = hidden // FF_TILE
    kept = {}

    def enter():
        load_cot.wait()
        load_out.wait()
        for tile in range(TILES):
            rows = pl.ds(tile * QT, QT)
            value = x_ref[rows, :].astype(F32) + mm(att_ref[rows, :], weight(0, D))
            h1_ref[rows, :] = value
            normed = (value * lax.rsqrt(mean_square(value) + EPSILON) * gain).astype(BF16)
            n_ref[rows, :] = normed
            ntt_ref[:, tile * QT : (tile + 1) * QT] = jnp.transpose(normed)
            gres_ref[rows, :] = (ga_ref[rows, :].astype(F32) * valid[tile * QT : (tile + 1) * QT]).astype(BF16)
        load_in.wait()
        load_down.wait()

    def inward(begin, end):
        def step(tile, carry):
            at = pl.multiple_of(tile * FF_TILE, FF_TILE)
            cols = pl.ds(at, FF_TILE)
            normed = n_ref[:ROWS, :]
            gate = mm(normed, weight(D + at, FF_TILE))
            up = mm(normed, weight(D + hidden + at, FF_TILE))
            back = mm_cols(gres_ref[...], wd_ref[cols, :])
            square = gate * gate
            bend = jnp.tanh(GELU_C * (gate * (1.0 + GELU_A * square)))
            half = 0.5 * (1.0 + bend)
            act = gate * half
            slope = half + (0.5 * GELU_C) * gate * (1.0 - bend * bend) * (1.0 + (3.0 * GELU_A) * square)
            b0_ref[:ROWS, cols] = (act * up).astype(BF16)
            b1_ref[:ROWS, cols] = (back * up * slope).astype(BF16)
            b2_ref[:ROWS, cols] = (back * act).astype(BF16)
            return carry

        lax.fori_loop(begin, end, step, 0)

    def outer_products(ref, right_ref, begin, end):
        def step(tile, carry):
            cols = pl.ds(pl.multiple_of(tile * FF_TILE, FF_TILE), FF_TILE)
            value = mm(ntt_ref[...], right_ref[:ROWS, cols]).astype(BF16)
            ref[:, :, :, cols] = value.reshape(outer, inner, part, FF_TILE)
            return carry

        lax.fori_loop(begin, end, step, 0)

    def down_products():
        def step(tile, carry):
            cols = pl.ds(pl.multiple_of(tile * FF_TILE, FF_TILE), FF_TILE)
            db_ref[tile // inner, tile % inner] = mm_rows(b0_ref[:ROWS, cols], gres_ref[...]).astype(BF16)
            return carry

        lax.fori_loop(0, tiles, step, 0)

    def outward():
        def step(tile, carry):
            cols = pl.ds(pl.multiple_of(tile * group, 128), group)
            value = h1_ref[:ROWS, cols] + mm(b0_ref[:ROWS, :hidden], wd_ref[:, cols])
            y_ref[:, cols] = (value * valid).astype(BF16)
            shards = pl.ds(tile * (4 // inner), 4 // inner)
            gh_ref[:, cols] = mm_cols(
                b1_ref[:ROWS, :hidden], wf_ref[shards, :, :, D : D + hidden].reshape(group, hidden)
            ) + mm_cols(b2_ref[:ROWS, :hidden], wf_ref[shards, :, :, D + hidden :].reshape(group, hidden))
            return carry

        lax.fori_loop(0, D // group, step, 0)
        kept["qkv"] = fetch(4, qkv_any, b1_ref)
        kept["wqkv"] = fetch(5, wqkv_any, b2_ref)

    def middle():
        gain_grad = jnp.zeros((1, D), F32)
        for tile in range(TILES):
            rows = pl.ds(tile * QT, QT)
            value, grad = h1_ref[rows, :], gh_ref[rows, :]
            root = lax.rsqrt(mean_square(value) + EPSILON)
            unit = value * root
            gain_grad = gain_grad + jnp.sum(grad * unit, axis=0, keepdims=True)
            grad = grad * gain
            grad = gres_ref[rows, :].astype(F32) + root * (
                grad - unit * jnp.mean(grad * unit, axis=-1, keepdims=True)
            )
            gh_ref[rows, :] = grad
            low = grad.astype(BF16)
            n_ref[rows, :] = low
            ga_ref[rows, :] = mm_cols(low, weight(0, D)).astype(BF16)
        kept["gain"] = gain_grad

    def out_products():
        def step(tile, carry):
            cols = pl.ds(pl.multiple_of(tile * QUAD, QUAD), QUAD)
            value = mm_rows(att_ref[...], n_ref[:ROWS, cols]).astype(BF16)
            do_ref[:, :, :, cols] = value.reshape(outer, inner, part, QUAD)
            return carry

        lax.fori_loop(0, D // QUAD, step, 0)
        kept["n"] = fetch(6, n_any, n_ref)

    def attention(quad):
        if quad == 0:
            backward_attention_start(dk_ref, dv_ref)
            kept["qkv"].wait()
        backward_attention_quad(tab_ref, rank, b1_ref, att_ref, ga_ref, lse_ref, b0_ref, dk_ref, dv_ref, quad)

    def project_products(quad):
        if quad == 0:
            kept["n"].wait()
        for number in range(3):
            value = mm_rows(n_ref[...], b0_ref[:, number * D + quad * QUAD : number * D + (quad + 1) * QUAD])
            low = (quad * 3 + number) * QUAD
            wf_ref[:, :, :, low : low + QUAD] = value.astype(BF16).reshape(outer, inner, part, QUAD)

    def input_gradient():
        kept["wqkv"].wait()
        kept["one"], kept["side"] = backward_project(
            tab_ref, rank, x_ref, gh_ref, gains, n_ref, b0_ref, b2_ref, dk_ref, gres_ref
        )

    def gain_pieces():
        rows = jnp.concatenate([kept["one"], kept["side"], kept["gain"], jnp.zeros((5, D), F32)], axis=0)
        spread_gain_grads(rows, dc_ref)

    half = tiles // 2
    work = {
        "start": lambda: None, "P0": enter, "P1a": lambda: inward(0, half), "P1b": lambda: inward(half, tiles),
        "gA": lambda: outer_products(dg_ref, b1_ref, 0, half), "gB": lambda: outer_products(dg_ref, b1_ref, half, tiles),
        "uA": lambda: outer_products(du_ref, b2_ref, 0, half), "uB": lambda: outer_products(du_ref, b2_ref, half, tiles),
        "d": down_products, "out": outward, "P4": middle, "P5": out_products,
        "q0": lambda: attention(0), "q1": lambda: attention(1), "q2": lambda: attention(2),
        "p0": lambda: project_products(0), "p1": lambda: project_products(1), "p2": lambda: project_products(2),
        "bp": input_gradient, "dc": gain_pieces,
    }
    paired = set()
    for action, which, *turn in REAR_ORDER:
        if action == "do":
            work[which]()
        elif action == "begin":
            if which == 6:
                pl.semaphore_wait(free_sem, 1)
            tasks[which].begin()
        elif action == "pair":
            tasks[which].pair()
            paired.add(which)
            if which < 3 and paired >= {0, 1, 2}:
                pl.semaphore_signal(free_sem, inc=1, device_id={"rep": links.mate}, device_id_type=MESH)
        elif action == "meet":
            tasks[which].meet()
        elif action == "col":
            tasks[which].column()
        elif action == "hop":
            tasks[which].hop(turn[0])
        elif action == "cross":
            tasks[which].cross()
        elif action == "fin":
            tasks[which].finish()
        elif action == "rows":
            returns[which].begin()
        else:
            returns[which].relay()
    for one in returns:
        one.settle()
    for task in tasks:
        task.settle()
    links.drain()


def feed_and_reduce(count, table, x, att, lse, gc, cot, n, qkv, wqkv, wf, wd):
    outer, inner = grid_of(count)
    part, tall = D // count, wd.shape[1]
    hidden = count * tall
    wf = wf.reshape((outer, inner) + wf.shape[1:])
    full = [(part, hidden), (part, hidden), (tall, D), (part, D), (part, 3 * D), (8, 128)]
    shapes = [(part, hidden // 2)] * 4 + [(tall, D)] + [(part, D)] * 4 + [(8, 128)]
    kinds = len(shapes)
    dtypes = [BF16] * (kinds - 1) + [F32]
    halved = [(a, b // 2 if b % 256 == 0 else b) for a, b in shapes]
    later = [(a // 2, b) if i in ACROSS_FIRST else (a, b) for i, (a, b) in enumerate(halved)]
    dma, vmem = pltpu.SemaphoreType.DMA, pltpu.VMEM
    scratch = [
        vmem((ROWS, D), BF16), vmem((ROWS, D), F32), vmem((ALL_ROWS, D), F32), vmem((ALL_ROWS, D), F32),
        vmem((ALL_ROWS, 3 * D), BF16), vmem((ALL_ROWS, 3 * D), BF16), vmem((D, 3 * D), BF16),
        vmem((ALL_ROWS, D), BF16), vmem((D, ROWS), BF16), vmem((ROWS, D), BF16), vmem((ROWS, D), BF16),
        vmem(wf.shape, BF16), vmem((hidden, D), BF16),
    ]
    scratch += [vmem((outer, inner) + shape, BF16) for shape in full[:4]]
    scratch += [vmem((outer, inner) + full[-1], F32)] * 2
    scratch += [vmem((outer, inner) + halved[i], dtypes[i]) for i in (0, 1, 2, 3, 4, 5, 9)]
    for lead in ((outer,), (outer + 1,), ()):
        for i in range(kinds):
            across = (outer, inner) if i in ACROSS_FIRST and lead == () else lead
            scratch.append(vmem(across + later[i], dtypes[i]))
    scratch += [vmem(shape, F32) for shape in later]
    for i in ACROSS_FIRST:
        scratch += [vmem(later[i], BF16), vmem(later[i], F32)]
    one = dma((kinds,))
    scratch += [one, one, one, one, one, dma((2, outer, kinds)), dma((outer + 1, kinds))] + [one] * 9
    scratch += [dma((2, 3)), dma((2, 3)), dma((2,)), dma((1,)), dma((7,)), pltpu.SemaphoreType.REGULAR]
    rows = jax.ShapeDtypeStruct((4, ROWS, D), BF16)
    outs = pl.pallas_call(
        partial(rear_kernel, outer, inner),
        out_shape=tuple(jax.ShapeDtypeStruct(shape, F32) for shape in full) + (rows, rows),
        in_specs=[SMEM] + [VMEM] * 4 + [ANY] * 6,
        out_specs=(ANY,) * 8,
        scratch_shapes=scratch,
        compiler_params=pltpu.CompilerParams(
            collective_id=2, has_side_effects=True, vmem_limit_bytes=67043328
        ),
        name="feed_and_reduce",
    )(table, x, att, lse, gc, cot, n, qkv, wqkv, wf, wd.reshape(hidden, D))
    return outs[:6], outs[6], outs[7]


def place_kernel(part, tab_ref, ry_ref, rg_ref, og_ref, ou_ref, od_ref, oo_ref, op_ref, oc_ref, *refs):
    (y_ref, g_ref, q_out, k_out, v_out, o_out, g_out, u_out, d_out, one_out, side_out, two_out), refs = refs[:12], refs[12:]
    (y_buf, g_buf, bg, bu, bd, bo, bp, sem_in, sem_out, sem_rows, sem_home) = refs
    blocks = y_buf.shape[0]
    base = lax.axis_index("rep") * blocks
    tables = ((og_ref, bg), (ou_ref, bu), (od_ref, bd), (oo_ref, bo), (op_ref, bp))
    reads = [pltpu.make_async_copy(src, dst, sem_in.at[i]) for i, (src, dst) in enumerate(tables)]
    rows = ((ry_ref, y_buf, y_ref), (rg_ref, g_buf, g_ref))

    def fetch(block, carry):
        index = tab_ref[48, base + block]
        safe = jnp.maximum(index, 0)
        for kind, (src, buf, _) in enumerate(rows):
            @pl.when(index >= 0)
            def _():
                pltpu.make_async_copy(
                    src.at[lax.div(safe, SLOTS), lax.rem(safe, SLOTS)], buf.at[block], sem_rows.at[kind, block]
                ).start()

            @pl.when(index < 0)
            def _():
                buf[block] = jnp.zeros(buf.shape[1:], buf.dtype)

        return carry

    lax.fori_loop(0, blocks, fetch, 0)
    for read in reads:
        read.start()

    def leave(block, carry):
        index = tab_ref[48, base + block]
        for kind, (src, buf, dst) in enumerate(rows):
            @pl.when(index >= 0)
            def _():
                pltpu.make_async_copy(src.at[0, 0], buf.at[block], sem_rows.at[kind, block]).wait()

            pltpu.make_async_copy(buf.at[block], dst.at[block], sem_home.at[kind, block]).start()
        return carry

    lax.fori_loop(0, blocks, leave, 0)
    for number, out in enumerate((one_out, side_out, two_out)):
        out[...] = oc_ref[number, :part]
    writes = []
    for number, (buf, dst) in enumerate(((bg, g_out), (bu, u_out), (bd, d_out), (bo, o_out))):
        reads[number].wait()
        writes.append(pltpu.make_async_copy(buf, dst, sem_out.at[number]))
        writes[-1].start()
    reads[4].wait()
    for quad in range(D // QUAD):
        for number, dst in enumerate((q_out, k_out, v_out)):
            low = (3 * quad + number) * QUAD
            copy = pltpu.make_async_copy(
                bp.at[:, low : low + QUAD], dst.at[:, quad * QUAD : (quad + 1) * QUAD], sem_out.at[4 + 3 * quad + number]
            )
            copy.start()
            writes.append(copy)
    for write in writes:
        write.wait()

    def rest(block, carry):
        for kind, (_, buf, dst) in enumerate(rows):
            pltpu.make_async_copy(buf.at[block], dst.at[block], sem_home.at[kind, block]).wait()
        return carry

    lax.fori_loop(0, blocks, rest, 0)


def place_all(table, ry, rg, totals, blocks, part, shape):
    out = jax.ShapeDtypeStruct
    og, ou, od, oo, op, oc = totals
    block = (blocks,) + ry.shape[2:]
    dma, vmem = pltpu.SemaphoreType.DMA, pltpu.VMEM
    gain = out((part,), F32)
    y, g, q, k, v, o, gate, up, down, one, side, two = pl.pallas_call(
        partial(place_kernel, part),
        out_shape=(out(block, ry.dtype), out(block, rg.dtype), out(oo.shape, F32), out(oo.shape, F32), out(oo.shape, F32),
                   out(oo.shape, F32), out(og.shape, F32), out(ou.shape, F32), out(od.shape, F32), gain, gain, gain),
        in_specs=[SMEM] + [ANY] * 7 + [VMEM],
        out_specs=(ANY,) * 9 + (VMEM,) * 3,
        scratch_shapes=[vmem(block, ry.dtype), vmem(block, rg.dtype)] + [vmem(t.shape, F32) for t in totals[:5]]
        + [dma((5,)), dma((13,)), dma((2, blocks)), dma((2, blocks))],
        compiler_params=pltpu.CompilerParams(vmem_limit_bytes=VMEM_LIMIT),
        name="place_outputs",
    )(table, ry, rg, og, ou, od, oo, op, oc)
    return (y.reshape(shape), g.reshape(shape), one, side, q, k, v, o, two, gate, up, down)


def per_device(count, layer_input, cotangent, lengths, attn_gain, global_gain, query_weight, key_weight,
               value_weight, out_weight, ffn_gain, gate_weight, up_weight, down_weight):
    micro, span, width = layer_input.shape
    hidden = gate_weight.shape[1]
    blocks = micro * span // BLK
    part = attn_gain.shape[0]
    rows_in = layer_input.reshape(blocks, BLK, width)
    cots_in = cotangent.reshape(blocks, BLK, width)
    weights = (query_weight, key_weight, value_weight, out_weight, gate_weight, up_weight)
    wc = jnp.pad(jnp.stack([attn_gain, global_gain, ffn_gain]), ((0, 13), (0, 128 - part)))
    if grid_of(count)[1] == 2 and part % 16 == 0:
        lens = lax.dynamic_update_slice(
            jnp.zeros((8, 128), jnp.int32), lengths.reshape(1, blocks), (0, lax.axis_index("rep") * blocks)
        )
        table, x, cot, n, qkv, att, lse, wqkv, gc, ga, gb = gather_and_attend(
            count, lens, rows_in, cots_in, weights, down_weight, wc
        )
        totals, ry, rg = feed_and_reduce(count, table, x, att, lse, gc, cot, n, qkv, wqkv, ga, gb)
        ry, rg = (rows.reshape(4, SLOTS, BLK, width) for rows in (ry, rg))
        return place_all(table, ry, rg, totals, blocks, part, layer_input.shape)
    else:
        table = deal_table(lengths)
        splits = ((0, 4 * width), (4 * width, 2 * hidden))
        ga, gb, gc, rows, cots = gather_weights(
            count, splits, table, rows_in, cots_in, jnp.concatenate(weights, axis=1), down_weight, wc
        )
        x, full = rows.reshape(ROWS, width), ga.reshape(width, -1)
        n, qkv, att, lse = attend(table, x, gc, full)
        y, gh, gatt, dg, du, db, do, gain = feed(
            table, x, cots.reshape(ROWS, width), att, gc, full, gb.reshape(-1, width)
        )
        g, dw, dc = backward_layer(table, x, gh, gatt, att, lse, n, qkv, gain, gc, full)
        grads = [grad.reshape(count, -1, grad.shape[-1]) for grad in (dg, du, db, do, dw, dc)]
        og, ou, ob, oo, ow, oc, ry, rg = reduce_grads(
            count, grads, y.reshape(SLOTS, BLK, width), g.reshape(SLOTS, BLK, width)
        )
        oq, ok, ov = ow[:, :width], ow[:, width : 2 * width], ow[:, 2 * width :]
    y_home, g_home = bring_home(table, ry, rg, blocks)
    return (
        y_home.reshape(layer_input.shape), g_home.reshape(layer_input.shape),
        oc[0, :part], oc[1, :part], oq, ok, ov, oo, oc[2, :part], og, ou, ob,
    )


def solution(mesh):
    rows = P(None, ("rep", "fsdp"), None)
    vector, matrix = P("fsdp"), P("fsdp", None)
    return jax.shard_map(
        partial(per_device, mesh.shape["fsdp"]),
        mesh=mesh,
        in_specs=(rows, rows, P(None, ("rep", "fsdp")), vector, vector, matrix, matrix, matrix, matrix,
                  vector, matrix, matrix, matrix),
        out_specs=(rows, rows, vector, vector, matrix, matrix, matrix, matrix, vector, matrix, matrix, matrix),
        check_vma=False,
    )
```

profile of v0, /device:TPU:0, one launch (start us, length us, event | category | flops | bytes accessed | tf_op | source)
XLA Modules:
  0.0 203.1 jit_solution(16695252329575496190)
XLA Ops:
  0.6 0.8 reshape.51
  1.4 1.3 fusion.8.refs_10_
  2.7 0.1 dynamic_update_slice.3.refs_0_
  2.8 0.0 copy-start
  2.8 0.6 copy-done
  3.4 81.7 %gather_and_attend.1 = (s32[56,128]{1,0:T(8,128)}, bf16[640,768]{1,0:T(8,128)(2,1)}, bf16[640,768]{1,0:T(8,128)(2,1)}, bf16[688,768]{1,0:T(8,128)(2,1)}, bf16[68...) custom-call(s32[8,128]{1,0:T(8,128)} %copy-done, ...), custom_call_target="tpu_custom_call" | custom-call | tf_op jit(solution)/shard_map/gather_and_attend/pallas_call | solution.py:1811
  85.1 108.7 %feed_and_reduce.1 = (f32[96,2048]{1,0:T(8,128)}, f32[96,2048]{1,0:T(8,128)}, f32[256,768]{1,0:T(8,128)}, f32[96,768]{1,0:T(8,128)}, f32[96,2304]{1,0:T(8,128)},...) custom-call(s32[56,128]{1,0:T(8,128)} %get-tuple-element.43.refs_0_.tab_ref, ...), custom_call_target="tpu_custom_call" | custom-call | tf_op jit(solution)/shard_map/feed_and_reduce/pallas_call | solution.py:2107
  193.8 9.1 %place_outputs.1 = (bf16[24,64,768]{2,1,0:T(8,128)(2,1)}, bf16[24,64,768]{2,1,0:T(8,128)(2,1)}, f32[96,768]{1,0:T(8,128)}, f32[96,768]{1,0:T(8,128)}, f32[96,768...) custom-call(s32[56,128]{1,0:T(8,128)} %get-tuple-element.43.refs_0_., ...), custom_call_target="tpu_custom_call" | custom-call | tf_op jit(solution)/shard_map/place_outputs/pallas_call | solution.py:2194
  (1 shorter events, 0.0 us)
Async XLA Ops:
  2.8 0.6 copy-start
where the time goes:
time: 203 us
  Pallas kernels  199 us (98%)
    pallas_call x1, Pallas kernels, feed_and_reduce(): pl.pallas_call(partial(rear_kernel, outer, inner), out_shape=tuple((jax.S...  109 us
    pallas_call x1, Pallas kernels, gather_and_attend(): pl.pallas_call(partial(front_kernel, outer, inner), out_shape=(shape((TAB...  81.7 us
    pallas_call x1, Pallas kernels, place_all(): pl.pallas_call(partial(place_kernel, part), out_shape=(out(block, ry.dtyp...  9.06 us

commit v1 on v0

--- a/solution.py
+++ b/solution.py
@@ -1165,7 +1165,7 @@
         self.mate, self.across = core_of(self.rank), across_of(self.rank)
         self.late = []
 
-    def greet(self, everyone=False):
+    def greet(self, everyone=False, later=False):
         barrier = pltpu.get_barrier_semaphore()
         neighbours = (
             (self.row + 1 < self.outer, {"fsdp": self.spot + self.inner}),
@@ -1184,7 +1184,9 @@
 
         for device in group:
             pl.semaphore_signal(barrier, inc=1, device_id={"rep": device}, device_id_type=MESH)
-        pl.semaphore_wait(barrier, amount)
+        self.met = lambda: pl.semaphore_wait(barrier, amount)
+        if not later:
+            self.met()
 
     def send(self, there, src, dst, ssem, rsem, device):
         def describe():
@@ -1486,22 +1488,23 @@
     tabv_ref[48:] = where
 
 
+ROW_FIRST = (3,)
 FRONT_ORDER = (
-    ("own", 5), ("own", 0), ("own", 1), ("own", 2), ("do", "table"), ("hop", 5, 0), ("pack", 0, 1), ("pack", 1, 1),
-    ("cross", 0), ("pack", 0, 0), ("hop", 0, 0), ("hop", 5, 1), ("cross", 1), ("pack", 1, 0), ("hop", 1, 0),
-    ("hop", 2, 0), ("hop", 0, 1), ("hop", 5, 2), ("hop", 1, 1), ("own", 3), ("hop", 2, 1), ("own", 4), ("hop", 0, 2),
-    ("hop", 1, 2), ("hop", 3, 0), ("fr", 5), ("rfin", 0), ("do", "norm"), ("hop", 2, 2), ("hop", 4, 0),
-    ("hop", 3, 1), ("fr", 0), ("hop", 4, 1), ("got", 0), ("do", "proj"), ("hop", 3, 2), ("fr", 1), ("do", "a0"),
-    ("hop", 4, 2), ("fr", 2), ("do", "a1"), ("rfin", 1), ("do", "a2"), ("fr", 3), ("xin", 1), ("fr", 4), ("got", 1),
-    ("got", 2), ("got", 3), ("got", 4),
+    ("own", 1), ("own", 3), ("do", "table"), ("hop", 1, 0), ("own", 0), ("pack", 0, 1), ("own", 5), ("hop", 1, 1),
+    ("pack", 0, 0), ("cross", 0), ("hop", 5, 0), ("yz", 3), ("hop", 0, 0), ("hop", 5, 1), ("hop", 1, 2), ("own", 4),
+    ("hop", 0, 1), ("pack", 1, 0), ("own", 2), ("hop", 5, 2), ("hop", 0, 2), ("fr", 1), ("hop", 2, 0),
+    ("pack", 1, 1), ("hop", 4, 0), ("rfin", 0), ("hop", 2, 1), ("cross", 1), ("fr", 0), ("fr", 5), ("do", "norm"),
+    ("hop", 4, 1), ("hop", 3, 0), ("got", 0), ("do", "proj"), ("hop", 2, 2), ("do", "a0"), ("xin", 1), ("hop", 4, 2),
+    ("do", "a1"), ("hop", 3, 1), ("fr", 2), ("do", "a2"), ("hop", 3, 2), ("fr", 4), ("rfin", 1),
 )
 
 
 def front_kernel(outer, inner, *refs):
-    (lens_ref, rows_any, cots_any, *weights), refs = refs[:9], refs[9:]
-    (wd_ref, wc_ref), refs = refs[:2], refs[2:]
-    tab_ref, outs_any, (ga_ref, gb_ref), refs = refs[0], refs[1:9], refs[9:11], refs[11:]
+    (raw_ref, rows_any, cots_any, *weights), refs = refs[:9], refs[9:]
+    (wd_any, *gain_refs), refs = refs[:4], refs[4:]
+    (tab_ref, gains_ref), outs_any, (ga_ref, gb_ref), refs = refs[:2], refs[2:9], refs[9:11], refs[11:]
     (stage, lens_all, tabs, psend, precv, xsend, xrecv, rows_ref, cots_ref), refs = refs[:9], refs[9:]
+    (lens_ref, wd_ref, wc_ref), refs = refs[:3], refs[3:]
     held, refs = refs[:8], refs[8:]
     x_ref, cot_ref, n_ref, qkv_ref, att_ref, lse_ref, wqkv_ref, gc_ref = held
     (l_send, l_recv, t_sem, w_sem, z_send, z_recv, y_send, y_recv, c_send, c_recv, d_send, d_recv, own_sem,
@@ -1517,11 +1520,13 @@
     tall = wd_ref.shape[0]
     hidden = weights[-1].shape[1]
     rest = stage.shape[1] - width
-    cuts = [0, 7 * rest // 19, 13 * rest // 19, rest]
+    cuts = [0, 7 * rest // 19, 11 * rest // 19, rest]
     spans = [(cuts[i], (cuts[i + 1] - cuts[i]) // 2) for i in range(3)]
 
     at = 0
     loads = []
+    loads.append(pltpu.make_async_copy(wd_any, wd_ref, w_sem.at[8]))
+    loads[0].start()
     row_loads = [pltpu.make_async_copy(rows_any, rows_ref, w_sem.at[6]), pltpu.make_async_copy(cots_any, cots_ref, w_sem.at[7])]
     for number, ref in enumerate(weights):
         cols = slice(at, at + ref.shape[1])
@@ -1531,6 +1536,22 @@
     for load in row_loads:
         load.start()
 
+    wc_ref[...] = jnp.zeros(wc_ref.shape, wc_ref.dtype)
+    for number, ref in enumerate(gain_refs):
+        wc_ref[number : number + 1, :part] = ref[...].reshape(1, part)
+    micro, spots = raw_ref.shape
+    lens_ref[...] = jnp.zeros(lens_ref.shape, lens_ref.dtype)
+    lens_ref[:micro, :spots] = raw_ref[...]
+    raw = lens_ref[...]
+    spread = jnp.zeros((1, 128), jnp.int32)
+    for device in range(4):
+        line = jnp.zeros((1, 128), jnp.int32)
+        for number in range(micro):
+            shift = device * micro * spots + number * spots
+            moved = raw if shift == 0 else pltpu.roll(raw, shift, 1)
+            line = line + moved[number : number + 1]
+        spread = jnp.where(rank == device, line, spread)
+    lens_ref[...] = jnp.broadcast_to(spread, (8, 128))
     links.greet(True)
     lens_all[rank] = lens_ref[...]
     for step in range(1, 4):
@@ -1596,23 +1617,37 @@
         return ((row - 1 - step >= 0, row - 1 - step, 0, row + 1 < outer, spot + inner),
                 (row + 1 + step < outer, row + 1 + step, 1, row > 0, spot - inner))
 
+    def along_line(number, column, src):
+        here = place(number, row * inner + (col if column == 0 else 1 - col))
+        src = here if src is None else src
+        links.send(row + 1 < outer, src, here, z_send.at[0, 0, number, column], z_recv.at[0, 0, number, column],
+                   {"fsdp": spot + inner})
+        links.send(row > 0, src, here, z_send.at[1, 0, number, column], z_recv.at[1, 0, number, column],
+                   {"fsdp": spot - inner})
+
     def own(number):
-        src, dst = source(number), place(number, spot)
-        links.send(row + 1 < outer, src, dst, z_send.at[0, 0, number], z_recv.at[0, 0, number],
-                   {"fsdp": spot + inner})
-        links.send(row > 0, src, dst, z_send.at[1, 0, number], z_recv.at[1, 0, number], {"fsdp": spot - inner})
+        src = source(number)
+        along_line(number, 0, src)
         along_row(None, number, row, src)
+
+    def second_column(number):
+        shard = row * inner + 1 - col
+        links.arrive(place(number, shard), y_recv.at[row, number], nobody)
+        share(None, number, shard)
+        along_line(number, 1, None)
 
     def hop(number, step):
         for here, line, way, onward, target in lines(step):
-            shard = line * inner + col
-            guarded(here, lambda: links.arrive(place(number, shard), z_recv.at[way, step, number], nobody))
-            if step + 1 < outer - 1:
-                view = place(number, shard)
-                links.send(both(here, onward), view, view, z_send.at[way, step + 1, number],
-                           z_recv.at[way, step + 1, number], {"fsdp": target})
-            along_row(here, number, line, None)
-            share(here, number, shard)
+            for column in range(2 if number in ROW_FIRST else 1):
+                shard = line * inner + (col if column == 0 else 1 - col)
+                guarded(here, lambda: links.arrive(place(number, shard), z_recv.at[way, step, number, column], nobody))
+                if step + 1 < outer - 1:
+                    view = place(number, shard)
+                    links.send(both(here, onward), view, view, z_send.at[way, step + 1, number, column],
+                               z_recv.at[way, step + 1, number, column], {"fsdp": target})
+                if number not in ROW_FIRST:
+                    along_row(here, number, line, None)
+                share(here, number, shard)
 
     def from_row(number):
         def one(there, line):
@@ -1738,8 +1773,10 @@
 
     def norm():
         keep[3].wait()
-        forward_norm(tabs, rank, x_ref, gains_of(gc_ref), n_ref)
-        leave(2, 7)
+        gains = gains_of(gc_ref)
+        gains_ref[...] = gains
+        forward_norm(tabs, rank, x_ref, gains, n_ref)
+        leave(2)
 
     def project():
         keep[0].wait()
@@ -1753,7 +1790,6 @@
 
     work = {"table": make_table, "norm": norm, "proj": project, "a0": lambda: attend_tiles(0, 2),
             "a1": lambda: attend_tiles(2, 4), "a2": lambda: attend_tiles(4, TILES)}
-    tail = []
     for action, which, *more in FRONT_ORDER:
         if action == "do":
             work[which]()
@@ -1763,12 +1799,12 @@
             hop(which, more[0])
         elif action == "fr":
             from_row(which)
+        elif action == "yz":
+            second_column(which)
         elif action == "xin":
             from_across()
-        elif action == "got" and which == 0:
-            gathered(0)
         elif action == "got":
-            tail.append(which)
+            gathered(which)
         elif action == "pack":
             pack_rows(which, more[0])
         elif action == "cross":
@@ -1776,7 +1812,7 @@
         else:
             finish_rows(which)
             leave(which)
-    gathered(*tail, 6)
+    gathered(1, 2, 3, 4, 6)
 
     def sent(shard, carry):
         @pl.when(shard != spot)
@@ -1798,31 +1834,31 @@
         copy.wait()
 
 
-def gather_and_attend(count, lens, rows, cots, weights, wd, wc):
+def gather_and_attend(count, lens, rows, cots, weights, wd, gains):
     outer, inner = grid_of(count)
     block = rows.shape[1:]
-    part, hidden = wd.shape[0], weights[-1].shape[1]
     part = weights[0].shape[0]
     dma, shape = pltpu.SemaphoreType.DMA, jax.ShapeDtypeStruct
     total = sum(weight.shape[1] for weight in weights)
     kinds = 6
     held = (shape((ROWS, D), BF16), shape((ROWS, D), BF16), shape((ALL_ROWS, D), BF16), shape((ALL_ROWS, 3 * D), BF16),
-            shape((ROWS, D), BF16), shape((TILES, 16, QT), F32), shape((D, 3 * D), BF16), shape((count,) + wc.shape, BF16))
+            shape((ROWS, D), BF16), shape((TILES, 16, QT), F32), shape((D, 3 * D), BF16))
     return pl.pallas_call(
         partial(front_kernel, outer, inner),
-        out_shape=(shape((TABLE_ROWS, 128), jnp.int32),) + held + (
+        out_shape=(shape((TABLE_ROWS, 128), jnp.int32), shape((16, D), F32)) + held + (
             shape((count, part, total - 3 * D), BF16), shape((count,) + wd.shape, BF16),
         ),
-        in_specs=[VMEM] + [ANY] * 8 + [VMEM] * 2,
-        out_specs=(VMEM,) + (ANY,) * 10,
+        in_specs=[VMEM] + [ANY] * 9 + [VMEM] * 3,
+        out_specs=(VMEM,) * 2 + (ANY,) * 9,
         scratch_shapes=[
             pltpu.VMEM((part, total), BF16), pltpu.VMEM((4, 8, 128), jnp.int32), pltpu.SMEM((TABLE_ROWS, 128), jnp.int32),
             pltpu.VMEM((2, 2, SLOTS) + block, BF16), pltpu.VMEM((2, 2, SLOTS) + block, BF16),
             pltpu.VMEM((2, SLOTS) + block, BF16), pltpu.VMEM((2, SLOTS) + block, BF16),
             pltpu.VMEM(rows.shape, BF16), pltpu.VMEM(cots.shape, BF16),
-            *(pltpu.VMEM(one.shape, one.dtype) for one in held),
-            dma((3,)), dma((3,)), dma((1,)), dma((8,)),
-            dma((2, outer - 1, kinds)), dma((2, outer - 1, kinds)), dma((outer, kinds)), dma((outer, kinds)),
+            pltpu.VMEM((8, 128), jnp.int32), pltpu.VMEM(wd.shape, BF16), pltpu.VMEM((16, 128), BF16),
+            *(pltpu.VMEM(one.shape, one.dtype) for one in held), pltpu.VMEM((count, 16, 128), BF16),
+            dma((3,)), dma((3,)), dma((1,)), dma((9,)),
+            dma((2, outer - 1, kinds, 2)), dma((2, outer - 1, kinds, 2)), dma((outer, kinds)), dma((outer, kinds)),
             dma((kinds + 1, count)), dma((kinds + 1, count)), dma((count,)), dma((count,)), dma((4,)),
             dma((2, 2)), dma((2, 2)), dma((2,)), dma((2,)), dma((1,)), dma((8,)),
         ],
@@ -1830,14 +1866,14 @@
             collective_id=1, has_side_effects=True, vmem_limit_bytes=VMEM_LIMIT
         ),
         name="gather_and_attend",
-    )(lens, rows, cots, *weights, wd, wc)
+    )(lens, rows, cots, *weights, wd, *gains)
 
 
 ACROSS_FIRST = (2, 3)
 REAR_ORDER = (
     ("do", "start"), ("do", "P0"), ("do", "P1a"), ("do", "gA"), ("begin", 0), ("do", "uA"), ("begin", 1),
     ("do", "P1b"), ("pair", 0), ("pair", 1), ("do", "gB"), ("begin", 2), ("do", "uB"), ("begin", 3), ("do", "d"),
-    ("begin", 4), ("pair", 2), ("pair", 3), ("do", "out"), ("rows", 0), ("pair", 4), ("col", 0), ("meet", 2),
+    ("begin", 4), ("pair", 2), ("pair", 3), ("do", "out"), ("do", "load"), ("rows", 0), ("pair", 4), ("col", 0), ("meet", 2),
     ("do", "P4"), ("col", 1), ("do", "P5"), ("begin", 5), ("do", "q0"), ("meet", 3), ("pair", 5), ("hop", 0, 1),
     ("hop", 1, 1), ("do", "p0"), ("begin", 6), ("do", "q1"), ("pair", 6), ("col", 4), ("hop", 0, 2), ("hop", 1, 2),
     ("do", "p1"), ("begin", 7), ("do", "q2"), ("pair", 7), ("col", 2), ("col", 3), ("hop", 0, 3), ("cross", 0),
@@ -1882,7 +1918,7 @@
     load_out = fetch(1, wf_any.at[:, :, :, :D], wf_ref.at[:, :, :, :D])
     load_in = fetch(2, wf_any.at[:, :, :, D:], wf_ref.at[:, :, :, D:])
     load_down = fetch(3, wd_any, wd_ref)
-    links.greet()
+    links.greet(later=True)
 
     def weight(start, size):
         return wf_ref[:, :, :, pl.ds(start, size)].reshape(D, size)
@@ -1903,7 +1939,7 @@
     for number, i in enumerate(ACROSS_FIRST):
         tasks[i].third, tasks[i].stage_two = extra[2 * number], extra[2 * number + 1]
     returns = (Return(links, y_ref, ry_ref, sems, 0), Return(links, gres_ref, rg_ref, sems, 1))
-    gains = gains_of(gc_ref)
+    gains = gc_ref[...]
     gain = gains[2:3]
     valid = valid_column(tab_ref, rank)
     h1_ref, dv_ref = fa_ref, fa_ref
@@ -1973,6 +2009,8 @@
             return carry
 
         lax.fori_loop(0, D // group, step, 0)
+
+    def load():
         kept["qkv"] = fetch(4, qkv_any, b1_ref)
         kept["wqkv"] = fetch(5, wqkv_any, b2_ref)
 
@@ -2030,7 +2068,7 @@
 
     half = tiles // 2
     work = {
-        "start": lambda: None, "P0": enter, "P1a": lambda: inward(0, half), "P1b": lambda: inward(half, tiles),
+        "start": lambda: None, "load": load, "P0": enter, "P1a": lambda: inward(0, half), "P1b": lambda: inward(half, tiles),
         "gA": lambda: outer_products(dg_ref, b1_ref, 0, half), "gB": lambda: outer_products(dg_ref, b1_ref, half, tiles),
         "uA": lambda: outer_products(du_ref, b2_ref, 0, half), "uB": lambda: outer_products(du_ref, b2_ref, half, tiles),
         "d": down_products, "out": outward, "P4": middle, "P5": out_products,
@@ -2038,11 +2076,14 @@
         "p0": lambda: project_products(0), "p1": lambda: project_products(1), "p2": lambda: project_products(2),
         "bp": input_gradient, "dc": gain_pieces,
     }
-    paired = set()
+    paired, begun = set(), set()
     for action, which, *turn in REAR_ORDER:
         if action == "do":
             work[which]()
         elif action == "begin":
+            if not begun:
+                links.met()
+            begun.add(which)
             if which == 6:
                 pl.semaphore_wait(free_sem, 1)
             tasks[which].begin()
@@ -2120,17 +2161,21 @@
 
 def place_kernel(part, tab_ref, ry_ref, rg_ref, og_ref, ou_ref, od_ref, oo_ref, op_ref, oc_ref, *refs):
     (y_ref, g_ref, q_out, k_out, v_out, o_out, g_out, u_out, d_out, one_out, side_out, two_out), refs = refs[:12], refs[12:]
-    (y_buf, g_buf, bg, bu, bd, bo, bp, sem_in, sem_out, sem_rows, sem_home) = refs
+    (y_buf, g_buf, zero, bg, bu, bd, bo, bp, sem_in, sem_out, sem_rows, sem_home) = refs
     blocks = y_buf.shape[0]
     base = lax.axis_index("rep") * blocks
     tables = ((og_ref, bg), (ou_ref, bu), (od_ref, bd), (oo_ref, bo), (op_ref, bp))
     reads = [pltpu.make_async_copy(src, dst, sem_in.at[i]) for i, (src, dst) in enumerate(tables)]
     rows = ((ry_ref, y_buf, y_ref), (rg_ref, g_buf, g_ref))
 
+    for read in reads:
+        read.start()
+    zero[...] = jnp.zeros(zero.shape, zero.dtype)
+
     def fetch(block, carry):
         index = tab_ref[48, base + block]
         safe = jnp.maximum(index, 0)
-        for kind, (src, buf, _) in enumerate(rows):
+        for kind, (src, buf, dst) in enumerate(rows):
             @pl.when(index >= 0)
             def _():
                 pltpu.make_async_copy(
@@ -2139,27 +2184,23 @@
 
             @pl.when(index < 0)
             def _():
-                buf[block] = jnp.zeros(buf.shape[1:], buf.dtype)
+                pltpu.make_async_copy(zero, dst.at[block], sem_home.at[kind, block]).start()
 
         return carry
 
     lax.fori_loop(0, blocks, fetch, 0)
-    for read in reads:
-        read.start()
-
-    def leave(block, carry):
-        index = tab_ref[48, base + block]
-        for kind, (src, buf, dst) in enumerate(rows):
-            @pl.when(index >= 0)
-            def _():
-                pltpu.make_async_copy(src.at[0, 0], buf.at[block], sem_rows.at[kind, block]).wait()
-
-            pltpu.make_async_copy(buf.at[block], dst.at[block], sem_home.at[kind, block]).start()
-        return carry
-
-    lax.fori_loop(0, blocks, leave, 0)
     for number, out in enumerate((one_out, side_out, two_out)):
         out[...] = oc_ref[number, :part]
+    def leave(block, carry):
+        @pl.when(tab_ref[48, base + block] >= 0)
+        def _():
+            for kind, (src, buf, dst) in enumerate(rows):
+                pltpu.make_async_copy(src.at[0, 0], buf.at[block], sem_rows.at[kind, block]).wait()
+                pltpu.make_async_copy(buf.at[block], dst.at[block], sem_home.at[kind, block]).start()
+
+        return carry
+
+    lax.fori_loop(0, blocks, leave, 0)
     writes = []
     for number, (buf, dst) in enumerate(((bg, g_out), (bu, u_out), (bd, d_out), (bo, o_out))):
         reads[number].wait()
@@ -2197,7 +2238,7 @@
                    out(oo.shape, F32), out(og.shape, F32), out(ou.shape, F32), out(od.shape, F32), gain, gain, gain),
         in_specs=[SMEM] + [ANY] * 7 + [VMEM],
         out_specs=(ANY,) * 9 + (VMEM,) * 3,
-        scratch_shapes=[vmem(block, ry.dtype), vmem(block, rg.dtype)] + [vmem(t.shape, F32) for t in totals[:5]]
+        scratch_shapes=[vmem(block, ry.dtype), vmem(block, rg.dtype), vmem(block[1:], ry.dtype)] + [vmem(t.shape, F32) for t in totals[:5]]
         + [dma((5,)), dma((13,)), dma((2, blocks)), dma((2, blocks))],
         compiler_params=pltpu.CompilerParams(vmem_limit_bytes=VMEM_LIMIT),
         name="place_outputs",
@@ -2214,19 +2255,17 @@
     rows_in = layer_input.reshape(blocks, BLK, width)
     cots_in = cotangent.reshape(blocks, BLK, width)
     weights = (query_weight, key_weight, value_weight, out_weight, gate_weight, up_weight)
-    wc = jnp.pad(jnp.stack([attn_gain, global_gain, ffn_gain]), ((0, 13), (0, 128 - part)))
+    gains = (attn_gain, global_gain, ffn_gain)
     if grid_of(count)[1] == 2 and part % 16 == 0:
-        lens = lax.dynamic_update_slice(
-            jnp.zeros((8, 128), jnp.int32), lengths.reshape(1, blocks), (0, lax.axis_index("rep") * blocks)
+        table, gains, x, cot, n, qkv, att, lse, wqkv, ga, gb = gather_and_attend(
+            count, lengths, rows_in, cots_in, weights, down_weight, gains
         )
-        table, x, cot, n, qkv, att, lse, wqkv, gc, ga, gb = gather_and_attend(
-            count, lens, rows_in, cots_in, weights, down_weight, wc
-        )
-        totals, ry, rg = feed_and_reduce(count, table, x, att, lse, gc, cot, n, qkv, wqkv, ga, gb)
+        totals, ry, rg = feed_and_reduce(count, table, x, att, lse, gains, cot, n, qkv, wqkv, ga, gb)
         ry, rg = (rows.reshape(4, SLOTS, BLK, width) for rows in (ry, rg))
         return place_all(table, ry, rg, totals, blocks, part, layer_input.shape)
     else:
         table = deal_table(lengths)
+        wc = jnp.pad(jnp.stack(gains), ((0, 13), (0, 128 - part)))
         splits = ((0, 4 * width), (4 * width, 2 * hidden))
         ga, gb, gc, rows, cots = gather_weights(
             count, splits, table, rows_in, cots_in, jnp.concatenate(weights, axis=1), down_weight, wc

time: 203 us -> 196 us (0.966)
  Pallas kernels: 199 us -> 195 us
    pallas_call x1, Pallas kernels: 81.7 us -> 78.6 us  [gather_and_attend(): pl.pallas_call(partial(front_kernel, outer, inner), out_shape=(shape((TAB...]
where the time goes in v1:
time: 196 us; the launch traced here: 195 us
  Pallas kernels  195 us (99%)
    pallas_call x1, Pallas kernels, feed_and_reduce(): pl.pallas_call(partial(rear_kernel, outer, inner), out_shape=tuple((jax.S...  108 us
    pallas_call x1, Pallas kernels, gather_and_attend(): pl.pallas_call(partial(front_kernel, outer, inner), out_shape=(shape((TAB...  78.6 us
    pallas_call x1, Pallas kernels, place_all(): pl.pallas_call(partial(place_kernel, part), out_shape=(out(block, ry.dtyp...  8.32 us

profile of v1, /device:TPU:0, one launch (start us, length us, event | category | flops | bytes accessed | tf_op | source)
XLA Modules:
  0.0 195.4 jit_solution(12477740758058491112)
XLA Ops:
  0.6 78.6 %gather_and_attend.1 = (s32[56,128]{1,0:T(8,128)}, f32[16,768]{1,0:T(8,128)}, bf16[640,768]{1,0:T(8,128)(2,1)}, bf16[640,768]{1,0:T(8,128)(2,1)}, bf16[688,768]{...) custom-call(s32[2,12]{1,0:T(2,128)} %refs_0_.1, ...), custom_call_target="tpu_custom_call" | custom-call | tf_op jit(solution)/shard_map/gather_and_attend/pallas_call | solution.py:1846
  79.3 107.7 %feed_and_reduce.1 = (f32[96,2048]{1,0:T(8,128)}, f32[96,2048]{1,0:T(8,128)}, f32[256,768]{1,0:T(8,128)}, f32[96,768]{1,0:T(8,128)}, f32[96,2304]{1,0:T(8,128)},...) custom-call(s32[56,128]{1,0:T(8,128)} %get-tuple-element.43.refs_0_.tab_ref, ...), custom_call_target="tpu_custom_call" | custom-call | tf_op jit(solution)/shard_map/feed_and_reduce/pallas_call | solution.py:2148
  186.9 8.3 %place_outputs.1 = (bf16[24,64,768]{2,1,0:T(8,128)(2,1)}, bf16[24,64,768]{2,1,0:T(8,128)(2,1)}, f32[96,768]{1,0:T(8,128)}, f32[96,768]{1,0:T(8,128)}, f32[96,768...) custom-call(s32[56,128]{1,0:T(8,128)} %get-tuple-element.43.refs_0_., ...), custom_call_target="tpu_custom_call" | custom-call | tf_op jit(solution)/shard_map/place_outputs/pallas_call | solution.py:2235

commit v2 on v1

--- a/solution.py
+++ b/solution.py
@@ -1080,6 +1080,14 @@
     return gain_grad, side_gain
 
 
+def gelu_both(gate):
+    square = gate * gate
+    bend = jnp.tanh(GELU_C * (gate * (1.0 + GELU_A * square)))
+    half = 0.5 * (1.0 + bend)
+    slope = half + (0.5 * GELU_C) * gate * (1.0 - bend * bend) * (1.0 + (3.0 * GELU_A) * square)
+    return gate * half, slope
+
+
 def first_kernel(tab_ref, x_ref, gc_ref, w_ref, n_ref, qkv_ref, att_ref, lse_ref):
     rank = lax.axis_index("rep")
     gains = gains_of(gc_ref)
@@ -1490,25 +1498,26 @@
 
 ROW_FIRST = (3,)
 FRONT_ORDER = (
-    ("own", 1), ("own", 3), ("do", "table"), ("hop", 1, 0), ("own", 0), ("pack", 0, 1), ("own", 5), ("hop", 1, 1),
-    ("pack", 0, 0), ("cross", 0), ("hop", 5, 0), ("yz", 3), ("hop", 0, 0), ("hop", 5, 1), ("hop", 1, 2), ("own", 4),
-    ("hop", 0, 1), ("pack", 1, 0), ("own", 2), ("hop", 5, 2), ("hop", 0, 2), ("fr", 1), ("hop", 2, 0),
-    ("pack", 1, 1), ("hop", 4, 0), ("rfin", 0), ("hop", 2, 1), ("cross", 1), ("fr", 0), ("fr", 5), ("do", "norm"),
-    ("hop", 4, 1), ("hop", 3, 0), ("got", 0), ("do", "proj"), ("hop", 2, 2), ("do", "a0"), ("xin", 1), ("hop", 4, 2),
-    ("do", "a1"), ("hop", 3, 1), ("fr", 2), ("do", "a2"), ("hop", 3, 2), ("fr", 4), ("rfin", 1),
+    ("own", 1), ("own", 3), ("do", "table"), ("hop", 1, 0), ("own", 0), ("pack", 0, 1), ("hop", 1, 1), ("own", 5),
+    ("cross", 0), ("own", 2), ("hop", 0, 0), ("hop", 1, 2), ("pack", 1, 1), ("pack", 0, 0), ("hop", 5, 0),
+    ("hop", 5, 1), ("hop", 5, 2), ("hop", 0, 1), ("yz", 3), ("hop", 0, 2), ("own", 4), ("cross", 1), ("fr", 1),
+    ("hop", 2, 0), ("pack", 1, 0), ("hop", 3, 0), ("fr", 5), ("rfin", 0), ("fr", 0), ("do", "norm"), ("hop", 2, 1),
+    ("got", 0), ("hop", 4, 0), ("do", "proj"), ("do", "a0"), ("hop", 2, 2), ("hop", 4, 1), ("hop", 3, 1),
+    ("do", "a1"), ("hop", 4, 2), ("fr", 2), ("do", "a2"), ("hop", 3, 2), ("got", 2), ("do", "enter"), ("rfin", 1),
+    ("fr", 4), ("xin", 1), ("got", 3), ("do", "half"),
 )
 
 
 def front_kernel(outer, inner, *refs):
     (raw_ref, rows_any, cots_any, *weights), refs = refs[:9], refs[9:]
     (wd_any, *gain_refs), refs = refs[:4], refs[4:]
-    (tab_ref, gains_ref), outs_any, (ga_ref, gb_ref), refs = refs[:2], refs[2:9], refs[9:11], refs[11:]
+    (tab_ref, gains_ref), outs_any, (ga_ref, gb_ref), refs = refs[:2], refs[2:16], refs[16:18], refs[18:]
     (stage, lens_all, tabs, psend, precv, xsend, xrecv, rows_ref, cots_ref), refs = refs[:9], refs[9:]
     (lens_ref, wd_ref, wc_ref), refs = refs[:3], refs[3:]
-    held, refs = refs[:8], refs[8:]
-    x_ref, cot_ref, n_ref, qkv_ref, att_ref, lse_ref, wqkv_ref, gc_ref = held
+    held, gc_ref, refs = refs[:14], refs[14], refs[15:]
+    x_ref, cot_ref, n_ref, qkv_ref, att_ref, lse_ref, wqkv_ref, w2_ref, h1_ref, nt_ref, ntt_ref, b0_ref, b1_ref, b2_ref = held
     (l_send, l_recv, t_sem, w_sem, z_send, z_recv, y_send, y_recv, c_send, c_recv, d_send, d_recv, own_sem,
-     p_send, p_recv, x_send, x_recv, spare, out_sem) = refs
+     p_send, p_recv, x_send, x_recv, spare, out_sem, piece_sem) = refs
     links = Links(outer, inner)
     rank, spot, core, mate, across = links.rank, links.spot, links.core, links.mate, links.across
     row, col = links.row, links.col
@@ -1520,19 +1529,22 @@
     tall = wd_ref.shape[0]
     hidden = weights[-1].shape[1]
     rest = stage.shape[1] - width
-    cuts = [0, 7 * rest // 19, 11 * rest // 19, rest]
-    spans = [(cuts[i], (cuts[i + 1] - cuts[i]) // 2) for i in range(3)]
+    half = hidden // 2
+    early = D + 2 * half
+    spans = [(0, (D + half) // 2), (D + half, half // 2), (early, half)]
 
     at = 0
     loads = []
-    loads.append(pltpu.make_async_copy(wd_any, wd_ref, w_sem.at[8]))
+    loads.append(pltpu.make_async_copy(wd_any, wd_ref, w_sem.at[2]))
     loads[0].start()
-    row_loads = [pltpu.make_async_copy(rows_any, rows_ref, w_sem.at[6]), pltpu.make_async_copy(cots_any, cots_ref, w_sem.at[7])]
-    for number, ref in enumerate(weights):
-        cols = slice(at, at + ref.shape[1])
-        loads.append(pltpu.make_async_copy(ref, stage.at[:, cols], w_sem.at[number]))
+    row_loads = [pltpu.make_async_copy(rows_any, rows_ref, w_sem.at[0]), pltpu.make_async_copy(cots_any, cots_ref, w_sem.at[1])]
+    parts = [(ref, slice(0, D)) for ref in weights[:4]]
+    parts += [(ref, cols) for cols in (slice(0, half), slice(half, hidden)) for ref in weights[4:]]
+    for number, (ref, cols) in enumerate(parts):
+        size = cols.stop - cols.start
+        loads.append(pltpu.make_async_copy(ref.at[:, cols], stage.at[:, at : at + size], w_sem.at[3 + number]))
         loads[-1].start()
-        at += ref.shape[1]
+        at += size
     for load in row_loads:
         load.start()
 
@@ -1573,8 +1585,8 @@
             return wd_ref.at[tall_rows(side), cols_of(0, down_half, core)]
         if number == 5:
             return wc_ref
-        start, half = spans[number - 2]
-        return stage.at[:, cols_of(width + start, half, core)]
+        start, size = spans[number - 2]
+        return stage.at[:, cols_of(width + start, size, core)]
 
     def place(number, shard, which=None):
         which = core if which is None else which
@@ -1584,8 +1596,10 @@
             return gb_ref.at[shard, tall_rows(side if number == 1 else 1 - side), cols_of(0, down_half, which)]
         if number == 5:
             return gc_ref.at[shard]
-        start, half = spans[number - 2]
-        return ga_ref.at[shard, :, cols_of(start, half, which)]
+        start, size = spans[number - 2]
+        if number == 4:
+            return ga_ref.at[shard, :, cols_of(0, size, which)]
+        return w2_ref.at[pl.ds(pl.multiple_of(shard * part, 16), part), cols_of(start, size, which)]
 
     nobody = spare.at[0]
 
@@ -1691,9 +1705,12 @@
         load.wait()
     keep = [
         pltpu.make_async_copy(stage.at[:, :width], wqkv_ref.at[pl.ds(pl.multiple_of(spot * part, 16), part)], own_sem.at[0]),
-        pltpu.make_async_copy(stage.at[:, width:], ga_ref.at[spot], own_sem.at[1]),
+        pltpu.make_async_copy(stage.at[:, width + early :], ga_ref.at[spot], own_sem.at[1]),
         pltpu.make_async_copy(wd_ref, gb_ref.at[spot], own_sem.at[2]),
         pltpu.make_async_copy(wc_ref, gc_ref.at[spot], own_sem.at[3]),
+        pltpu.make_async_copy(
+            stage.at[:, width : width + early], w2_ref.at[pl.ds(pl.multiple_of(spot * part, 16), part)], own_sem.at[4]
+        ),
     ]
     for copy in keep:
         copy.start()
@@ -1788,7 +1805,41 @@
         if end == TILES:
             leave(4, 5)
 
-    work = {"table": make_table, "norm": norm, "proj": project, "a0": lambda: attend_tiles(0, 2),
+    def enter():
+        gain = gains_ref[2:3]
+        for tile in range(TILES):
+            rows = pl.ds(tile * QT, QT)
+            value = x_ref[rows, :].astype(F32) + mm(att_ref[rows, :], w2_ref[:, :D])
+            h1_ref[rows, :] = value
+            normed = (value * lax.rsqrt(mean_square(value) + EPSILON) * gain).astype(BF16)
+            nt_ref[rows, :] = normed
+            ntt_ref[:, tile * QT : (tile + 1) * QT] = jnp.transpose(normed)
+        leave(8, 9, 10)
+
+    def first_half():
+        def step(tile, carry):
+            at = pl.multiple_of(tile * FF_TILE, FF_TILE)
+            cols = pl.ds(at, FF_TILE)
+            gate = mm(nt_ref[...], w2_ref[:, pl.ds(D + at, FF_TILE)])
+            up = mm(nt_ref[...], w2_ref[:, pl.ds(D + half + at, FF_TILE)])
+            act, slope = gelu_both(gate)
+            b0_ref[:, cols] = (act * up).astype(BF16)
+            b1_ref[:, cols] = (up * slope).astype(BF16)
+            b2_ref[:, cols] = act.astype(BF16)
+            for copy in piece_copies(tile):
+                copy.start()
+            return carry
+
+        lax.fori_loop(0, half // FF_TILE, step, 0)
+
+    def piece_copies(tile):
+        cols = pl.ds(pl.multiple_of(tile * FF_TILE, FF_TILE), FF_TILE)
+        return [
+            pltpu.make_async_copy(held[number].at[:, cols], outs_any[number].at[:, cols], piece_sem.at[number - 11, tile])
+            for number in (11, 12, 13)
+        ]
+
+    work = {"table": make_table, "enter": enter, "half": first_half, "norm": norm, "proj": project, "a0": lambda: attend_tiles(0, 2),
             "a1": lambda: attend_tiles(2, 4), "a2": lambda: attend_tiles(4, TILES)}
     for action, which, *more in FRONT_ORDER:
         if action == "do":
@@ -1805,6 +1856,10 @@
             from_across()
         elif action == "got":
             gathered(which)
+            if which == 2:
+                keep[4].wait()
+            if which == 3:
+                leave(7)
         elif action == "pack":
             pack_rows(which, more[0])
         elif action == "cross":
@@ -1812,7 +1867,7 @@
         else:
             finish_rows(which)
             leave(which)
-    gathered(1, 2, 3, 4, 6)
+    gathered(1, 4, 6)
 
     def sent(shard, carry):
         @pl.when(shard != spot)
@@ -1832,24 +1887,28 @@
         across_copy(kind).wait_send()
     for copy in keep[1:3] + leaving:
         copy.wait()
+    for tile in range(half // FF_TILE):
+        for copy in piece_copies(tile):
+            copy.wait()
 
 
 def gather_and_attend(count, lens, rows, cots, weights, wd, gains):
     outer, inner = grid_of(count)
     block = rows.shape[1:]
-    part = weights[0].shape[0]
+    part, hidden = weights[0].shape[0], weights[-1].shape[1]
     dma, shape = pltpu.SemaphoreType.DMA, jax.ShapeDtypeStruct
     total = sum(weight.shape[1] for weight in weights)
     kinds = 6
     held = (shape((ROWS, D), BF16), shape((ROWS, D), BF16), shape((ALL_ROWS, D), BF16), shape((ALL_ROWS, 3 * D), BF16),
-            shape((ROWS, D), BF16), shape((TILES, 16, QT), F32), shape((D, 3 * D), BF16))
+            shape((ROWS, D), BF16), shape((TILES, 16, QT), F32), shape((D, 3 * D), BF16), shape((D, D + hidden), BF16), shape((ROWS, D), F32),
+            shape((ROWS, D), BF16), shape((D, ROWS), BF16)) + (shape((ROWS, hidden // 2), BF16),) * 3
     return pl.pallas_call(
         partial(front_kernel, outer, inner),
         out_shape=(shape((TABLE_ROWS, 128), jnp.int32), shape((16, D), F32)) + held + (
-            shape((count, part, total - 3 * D), BF16), shape((count,) + wd.shape, BF16),
+            shape((count, part, hidden), BF16), shape((count,) + wd.shape, BF16),
         ),
         in_specs=[VMEM] + [ANY] * 9 + [VMEM] * 3,
-        out_specs=(VMEM,) * 2 + (ANY,) * 9,
+        out_specs=(VMEM,) * 2 + (ANY,) * 16,
         scratch_shapes=[
             pltpu.VMEM((part, total), BF16), pltpu.VMEM((4, 8, 128), jnp.int32), pltpu.SMEM((TABLE_ROWS, 128), jnp.int32),
             pltpu.VMEM((2, 2, SLOTS) + block, BF16), pltpu.VMEM((2, 2, SLOTS) + block, BF16),
@@ -1857,10 +1916,10 @@
             pltpu.VMEM(rows.shape, BF16), pltpu.VMEM(cots.shape, BF16),
             pltpu.VMEM((8, 128), jnp.int32), pltpu.VMEM(wd.shape, BF16), pltpu.VMEM((16, 128), BF16),
             *(pltpu.VMEM(one.shape, one.dtype) for one in held), pltpu.VMEM((count, 16, 128), BF16),
-            dma((3,)), dma((3,)), dma((1,)), dma((9,)),
+            dma((3,)), dma((3,)), dma((1,)), dma((11,)),
             dma((2, outer - 1, kinds, 2)), dma((2, outer - 1, kinds, 2)), dma((outer, kinds)), dma((outer, kinds)),
-            dma((kinds + 1, count)), dma((kinds + 1, count)), dma((count,)), dma((count,)), dma((4,)),
-            dma((2, 2)), dma((2, 2)), dma((2,)), dma((2,)), dma((1,)), dma((8,)),
+            dma((kinds + 1, count)), dma((kinds + 1, count)), dma((count,)), dma((count,)), dma((5,)),
+            dma((2, 2)), dma((2, 2)), dma((2,)), dma((2,)), dma((1,)), dma((14,)), dma((3, hidden // 2 // FF_TILE)),
         ],
         compiler_params=pltpu.CompilerParams(
             collective_id=1, has_side_effects=True, vmem_limit_bytes=VMEM_LIMIT
@@ -1869,31 +1928,33 @@
     )(lens, rows, cots, *weights, wd, *gains)
 
 
-ACROSS_FIRST = (2, 3)
+ACROSS_FIRST = (1, 2)
 REAR_ORDER = (
-    ("do", "start"), ("do", "P0"), ("do", "P1a"), ("do", "gA"), ("begin", 0), ("do", "uA"), ("begin", 1),
-    ("do", "P1b"), ("pair", 0), ("pair", 1), ("do", "gB"), ("begin", 2), ("do", "uB"), ("begin", 3), ("do", "d"),
-    ("begin", 4), ("pair", 2), ("pair", 3), ("do", "out"), ("do", "load"), ("rows", 0), ("pair", 4), ("col", 0), ("meet", 2),
-    ("do", "P4"), ("col", 1), ("do", "P5"), ("begin", 5), ("do", "q0"), ("meet", 3), ("pair", 5), ("hop", 0, 1),
-    ("hop", 1, 1), ("do", "p0"), ("begin", 6), ("do", "q1"), ("pair", 6), ("col", 4), ("hop", 0, 2), ("hop", 1, 2),
-    ("do", "p1"), ("begin", 7), ("do", "q2"), ("pair", 7), ("col", 2), ("col", 3), ("hop", 0, 3), ("cross", 0),
-    ("hop", 1, 3), ("cross", 1), ("do", "bp"), ("rows", 1), ("relay", 0), ("col", 5), ("hop", 4, 1), ("fin", 0),
-    ("fin", 1), ("do", "p2"), ("begin", 8), ("hop", 2, 1), ("do", "dc"), ("begin", 9), ("hop", 3, 1), ("pair", 8),
-    ("pair", 9), ("col", 6), ("hop", 4, 2), ("hop", 5, 1), ("hop", 2, 2), ("hop", 3, 2), ("hop", 6, 1),
-    ("hop", 5, 2), ("hop", 6, 2), ("hop", 4, 3), ("cross", 4), ("col", 7), ("hop", 7, 1), ("hop", 2, 3),
-    ("cross", 2), ("hop", 3, 3), ("cross", 3), ("col", 8), ("col", 9), ("hop", 5, 3), ("cross", 5), ("hop", 6, 3),
-    ("cross", 6), ("relay", 1), ("hop", 8, 1), ("hop", 9, 1), ("hop", 7, 2), ("hop", 8, 2), ("hop", 9, 2),
-    ("fin", 4), ("fin", 2), ("fin", 3), ("hop", 7, 3), ("cross", 7), ("fin", 5), ("hop", 8, 3), ("cross", 8),
-    ("hop", 9, 3), ("cross", 9), ("fin", 6), ("fin", 7), ("fin", 8), ("fin", 9),
+    ("do", "start"), ("do", "P0"), ("do", "P1a"), ("do", "gA"), ("begin", 0), ("do", "P1b"), ("pair", 0),
+    ("do", "gB"), ("begin", 2), ("do", "uB"), ("begin", 3), ("do", "d"), ("begin", 4), ("pair", 2), ("do", "uA"),
+    ("begin", 1), ("pair", 3), ("do", "out"), ("pair", 1), ("pair", 4), ("do", "load"), ("do", "P4"), ("do", "P5"),
+    ("col", 0), ("col", 3), ("rows", 0), ("do", "q0"), ("do", "q1"), ("hop", 0, 1), ("meet", 2), ("do", "q2"),
+    ("meet", 1), ("col", 4), ("do", "p0"), ("begin", 6), ("do", "bp"), ("rows", 1), ("pair", 6), ("do", "p1"),
+    ("hop", 3, 1), ("begin", 5), ("hop", 0, 2), ("begin", 7), ("do", "dc"), ("do", "p2"), ("begin", 8), ("col", 2),
+    ("pair", 7), ("hop", 4, 1), ("pair", 5), ("begin", 9), ("hop", 2, 1), ("col", 1), ("col", 6), ("hop", 0, 3),
+    ("hop", 4, 2), ("col", 7), ("hop", 3, 2), ("hop", 6, 1), ("cross", 0), ("hop", 1, 1), ("pair", 8), ("hop", 4, 3),
+    ("pair", 9), ("hop", 6, 2), ("col", 5), ("hop", 3, 3), ("cross", 4), ("cross", 3), ("hop", 7, 1), ("hop", 1, 2),
+    ("hop", 2, 2), ("hop", 5, 1), ("col", 8), ("hop", 1, 3), ("cross", 1), ("hop", 6, 3), ("hop", 5, 2), ("col", 9),
+    ("cross", 6), ("relay", 1), ("hop", 5, 3), ("cross", 5), ("hop", 2, 3), ("hop", 7, 2), ("hop", 7, 3),
+    ("cross", 2), ("hop", 8, 1), ("relay", 0), ("cross", 7), ("hop", 9, 1), ("hop", 8, 2), ("hop", 9, 2),
+    ("hop", 8, 3), ("cross", 8), ("fin", 2), ("fin", 4), ("hop", 9, 3), ("fin", 5), ("fin", 0), ("fin", 1),
+    ("cross", 9), ("fin", 7), ("fin", 3), ("fin", 6), ("fin", 8), ("fin", 9),
 )
 
 
 def rear_kernel(outer, inner, *refs):
-    (tab_ref, x_ref, att_ref, lse_ref, gc_ref), refs = refs[:5], refs[5:]
-    (cot_any, n_any, qkv_any, wqkv_any, wf_any, wd_any), refs = refs[:6], refs[6:]
+    (tab_ref, x_any, att_any, lse_ref, gc_ref), refs = refs[:5], refs[5:]
+    (cot_any, n_any, qkv_any, wqkv_any, w2_any, wf_any, wd_any), refs = refs[:7], refs[7:]
+    (h1_any, nt_any, ntt_any, b0_any, b1_any, b2_any), refs = refs[:6], refs[6:]
     kinds = 10
     (og_ref, ou_ref, od_ref, oo_ref, op_ref, oc_ref, ry_ref, rg_ref), refs = refs[:8], refs[8:]
     (y_ref, gh_ref, fa_ref, dk_ref, b0_ref, b1_ref, b2_ref, n_ref, ntt_ref, gres_ref, ga_ref), refs = refs[:11], refs[11:]
+    (x_ref, att_ref), refs = refs[:2], refs[2:]
     (wf_ref, wd_ref, dg_ref, du_ref, db_ref, do_ref, dc_ref, mine_ref), refs = refs[:8], refs[8:]
     crecv, refs = list(refs[:7]), refs[7:]
     narrow = D // 2
@@ -1914,16 +1975,22 @@
         copy.start()
         return copy
 
-    load_cot = fetch(0, cot_any, ga_ref)
-    load_out = fetch(1, wf_any.at[:, :, :, :D], wf_ref.at[:, :, :, :D])
-    load_in = fetch(2, wf_any.at[:, :, :, D:], wf_ref.at[:, :, :, D:])
-    load_down = fetch(3, wd_any, wd_ref)
+    wide, early = hidden // 2, D + hidden
+    load_first = [
+        fetch(0, cot_any, ga_ref), fetch(1, wd_any.at[:wide], wd_ref.at[:wide]),
+        fetch(7, b1_any, b1_ref.at[:ROWS, :wide]), fetch(8, b2_any, b2_ref.at[:ROWS, :wide]),
+    ]
+    load_products = fetch(9, ntt_any, ntt_ref)
+    load_rest = [
+        fetch(10, nt_any, n_ref.at[:ROWS]), fetch(2, wf_any, wf_ref.at[:, :, :, early:]),
+        fetch(3, wd_any.at[wide:], wd_ref.at[wide:]), fetch(11, b0_any, b0_ref.at[:ROWS, :wide]),
+        fetch(12, h1_any, fa_ref.at[:ROWS]), fetch(4, x_any, x_ref), fetch(5, att_any, att_ref), fetch(13, w2_any, wf_ref.at[:, :, :, :early]),
+    ]
     links.greet(later=True)
 
     def weight(start, size):
         return wf_ref[:, :, :, pl.ds(start, size)].reshape(D, size)
 
-    wide = hidden // 2
     first, second = slice(0, wide), slice(wide, hidden)
     grads = [dg_ref.at[:, :, :, first], du_ref.at[:, :, :, first], dg_ref.at[:, :, :, second], du_ref.at[:, :, :, second],
              db_ref, do_ref] + [wf_ref.at[:, :, :, i * D : (i + 1) * D] for i in range(3)] + [dc_ref]
@@ -1944,41 +2011,45 @@
     valid = valid_column(tab_ref, rank)
     h1_ref, dv_ref = fa_ref, fa_ref
     tiles = hidden // FF_TILE
+    half = tiles // 2
     kept = {}
 
     def enter():
-        load_cot.wait()
-        load_out.wait()
+        for load in load_first:
+            load.wait()
         for tile in range(TILES):
             rows = pl.ds(tile * QT, QT)
-            value = x_ref[rows, :].astype(F32) + mm(att_ref[rows, :], weight(0, D))
-            h1_ref[rows, :] = value
-            normed = (value * lax.rsqrt(mean_square(value) + EPSILON) * gain).astype(BF16)
-            n_ref[rows, :] = normed
-            ntt_ref[:, tile * QT : (tile + 1) * QT] = jnp.transpose(normed)
             gres_ref[rows, :] = (ga_ref[rows, :].astype(F32) * valid[tile * QT : (tile + 1) * QT]).astype(BF16)
-        load_in.wait()
-        load_down.wait()
-
-    def inward(begin, end):
+
+    def first_half():
+        def step(tile, carry):
+            cols = pl.ds(pl.multiple_of(tile * FF_TILE, FF_TILE), FF_TILE)
+            back = mm_cols(gres_ref[...], wd_ref[cols, :])
+            b1_ref[:ROWS, cols] = (back * b1_ref[:ROWS, cols].astype(F32)).astype(BF16)
+            b2_ref[:ROWS, cols] = (back * b2_ref[:ROWS, cols].astype(F32)).astype(BF16)
+            return carry
+
+        lax.fori_loop(0, half, step, 0)
+        load_products.wait()
+
+    def second_half():
+        for load in load_rest:
+            load.wait()
+
         def step(tile, carry):
             at = pl.multiple_of(tile * FF_TILE, FF_TILE)
             cols = pl.ds(at, FF_TILE)
             normed = n_ref[:ROWS, :]
-            gate = mm(normed, weight(D + at, FF_TILE))
-            up = mm(normed, weight(D + hidden + at, FF_TILE))
+            gate = mm(normed, weight(early - wide + at, FF_TILE))
+            up = mm(normed, weight(early + at, FF_TILE))
             back = mm_cols(gres_ref[...], wd_ref[cols, :])
-            square = gate * gate
-            bend = jnp.tanh(GELU_C * (gate * (1.0 + GELU_A * square)))
-            half = 0.5 * (1.0 + bend)
-            act = gate * half
-            slope = half + (0.5 * GELU_C) * gate * (1.0 - bend * bend) * (1.0 + (3.0 * GELU_A) * square)
+            act, slope = gelu_both(gate)
             b0_ref[:ROWS, cols] = (act * up).astype(BF16)
             b1_ref[:ROWS, cols] = (back * up * slope).astype(BF16)
             b2_ref[:ROWS, cols] = (back * act).astype(BF16)
             return carry
 
-        lax.fori_loop(begin, end, step, 0)
+        lax.fori_loop(half, tiles, step, 0)
 
     def outer_products(ref, right_ref, begin, end):
         def step(tile, carry):
@@ -2003,16 +2074,21 @@
             value = h1_ref[:ROWS, cols] + mm(b0_ref[:ROWS, :hidden], wd_ref[:, cols])
             y_ref[:, cols] = (value * valid).astype(BF16)
             shards = pl.ds(tile * (4 // inner), 4 // inner)
-            gh_ref[:, cols] = mm_cols(
-                b1_ref[:ROWS, :hidden], wf_ref[shards, :, :, D : D + hidden].reshape(group, hidden)
-            ) + mm_cols(b2_ref[:ROWS, :hidden], wf_ref[shards, :, :, D + hidden :].reshape(group, hidden))
+            total = None
+            for number, (ref, low) in enumerate(((b1_ref, 0), (b2_ref, 0), (b1_ref, wide), (b2_ref, wide))):
+                at = D + number * wide
+                term = mm_cols(
+                    ref[:ROWS, low : low + wide], wf_ref[shards, :, :, at : at + wide].reshape(group, wide)
+                )
+                total = term if total is None else total + term
+            gh_ref[:, cols] = total
             return carry
 
         lax.fori_loop(0, D // group, step, 0)
 
     def load():
-        kept["qkv"] = fetch(4, qkv_any, b1_ref)
-        kept["wqkv"] = fetch(5, wqkv_any, b2_ref)
+        kept["qkv"] = fetch(14, qkv_any, b1_ref)
+        kept["wqkv"] = fetch(15, wqkv_any, b2_ref)
 
     def middle():
         gain_grad = jnp.zeros((1, D), F32)
@@ -2066,9 +2142,8 @@
         rows = jnp.concatenate([kept["one"], kept["side"], kept["gain"], jnp.zeros((5, D), F32)], axis=0)
         spread_gain_grads(rows, dc_ref)
 
-    half = tiles // 2
     work = {
-        "start": lambda: None, "load": load, "P0": enter, "P1a": lambda: inward(0, half), "P1b": lambda: inward(half, tiles),
+        "start": lambda: None, "load": load, "P0": enter, "P1a": first_half, "P1b": second_half,
         "gA": lambda: outer_products(dg_ref, b1_ref, 0, half), "gB": lambda: outer_products(dg_ref, b1_ref, half, tiles),
         "uA": lambda: outer_products(du_ref, b2_ref, 0, half), "uB": lambda: outer_products(du_ref, b2_ref, half, tiles),
         "d": down_products, "out": outward, "P4": middle, "P5": out_products,
@@ -2113,11 +2188,12 @@
     links.drain()
 
 
-def feed_and_reduce(count, table, x, att, lse, gc, cot, n, qkv, wqkv, wf, wd):
+def feed_and_reduce(count, table, x, att, lse, gc, cot, n, qkv, wqkv, w2, wf, wd, *firsts):
     outer, inner = grid_of(count)
     part, tall = D // count, wd.shape[1]
     hidden = count * tall
     wf = wf.reshape((outer, inner) + wf.shape[1:])
+    w2 = w2.reshape(outer, inner, part, -1)
     full = [(part, hidden), (part, hidden), (tall, D), (part, D), (part, 3 * D), (8, 128)]
     shapes = [(part, hidden // 2)] * 4 + [(tall, D)] + [(part, D)] * 4 + [(8, 128)]
     kinds = len(shapes)
@@ -2129,7 +2205,8 @@
         vmem((ROWS, D), BF16), vmem((ROWS, D), F32), vmem((ALL_ROWS, D), F32), vmem((ALL_ROWS, D), F32),
         vmem((ALL_ROWS, 3 * D), BF16), vmem((ALL_ROWS, 3 * D), BF16), vmem((D, 3 * D), BF16),
         vmem((ALL_ROWS, D), BF16), vmem((D, ROWS), BF16), vmem((ROWS, D), BF16), vmem((ROWS, D), BF16),
-        vmem(wf.shape, BF16), vmem((hidden, D), BF16),
+        vmem((ROWS, D), BF16), vmem((ROWS, D), BF16),
+        vmem((outer, inner, part, D + 2 * hidden), BF16), vmem((hidden, D), BF16),
     ]
     scratch += [vmem((outer, inner) + shape, BF16) for shape in full[:4]]
     scratch += [vmem((outer, inner) + full[-1], F32)] * 2
@@ -2143,19 +2220,19 @@
         scratch += [vmem(later[i], BF16), vmem(later[i], F32)]
     one = dma((kinds,))
     scratch += [one, one, one, one, one, dma((2, outer, kinds)), dma((outer + 1, kinds))] + [one] * 9
-    scratch += [dma((2, 3)), dma((2, 3)), dma((2,)), dma((1,)), dma((7,)), pltpu.SemaphoreType.REGULAR]
+    scratch += [dma((2, 3)), dma((2, 3)), dma((2,)), dma((1,)), dma((16,)), pltpu.SemaphoreType.REGULAR]
     rows = jax.ShapeDtypeStruct((4, ROWS, D), BF16)
     outs = pl.pallas_call(
         partial(rear_kernel, outer, inner),
         out_shape=tuple(jax.ShapeDtypeStruct(shape, F32) for shape in full) + (rows, rows),
-        in_specs=[SMEM] + [VMEM] * 4 + [ANY] * 6,
+        in_specs=[SMEM] + [ANY] * 2 + [VMEM] * 2 + [ANY] * 13,
         out_specs=(ANY,) * 8,
         scratch_shapes=scratch,
         compiler_params=pltpu.CompilerParams(
             collective_id=2, has_side_effects=True, vmem_limit_bytes=67043328
         ),
         name="feed_and_reduce",
-    )(table, x, att, lse, gc, cot, n, qkv, wqkv, wf, wd.reshape(hidden, D))
+    )(table, x, att, lse, gc, cot, n, qkv, wqkv, w2, wf, wd.reshape(hidden, D), *firsts)
     return outs[:6], outs[6], outs[7]
 
 
@@ -2191,16 +2268,6 @@
     lax.fori_loop(0, blocks, fetch, 0)
     for number, out in enumerate((one_out, side_out, two_out)):
         out[...] = oc_ref[number, :part]
-    def leave(block, carry):
-        @pl.when(tab_ref[48, base + block] >= 0)
-        def _():
-            for kind, (src, buf, dst) in enumerate(rows):
-                pltpu.make_async_copy(src.at[0, 0], buf.at[block], sem_rows.at[kind, block]).wait()
-                pltpu.make_async_copy(buf.at[block], dst.at[block], sem_home.at[kind, block]).start()
-
-        return carry
-
-    lax.fori_loop(0, blocks, leave, 0)
     writes = []
     for number, (buf, dst) in enumerate(((bg, g_out), (bu, u_out), (bd, d_out), (bo, o_out))):
         reads[number].wait()
@@ -2215,6 +2282,16 @@
             )
             copy.start()
             writes.append(copy)
+    def leave(block, carry):
+        @pl.when(tab_ref[48, base + block] >= 0)
+        def _():
+            for kind, (src, buf, dst) in enumerate(rows):
+                pltpu.make_async_copy(src.at[0, 0], buf.at[block], sem_rows.at[kind, block]).wait()
+                pltpu.make_async_copy(buf.at[block], dst.at[block], sem_home.at[kind, block]).start()
+
+        return carry
+
+    lax.fori_loop(0, blocks, leave, 0)
     for write in writes:
         write.wait()
 
@@ -2257,10 +2334,10 @@
     weights = (query_weight, key_weight, value_weight, out_weight, gate_weight, up_weight)
     gains = (attn_gain, global_gain, ffn_gain)
     if grid_of(count)[1] == 2 and part % 16 == 0:
-        table, gains, x, cot, n, qkv, att, lse, wqkv, ga, gb = gather_and_attend(
+        table, gains, x, cot, n, qkv, att, lse, wqkv, w2, *firsts, ga, gb = gather_and_attend(
             count, lengths, rows_in, cots_in, weights, down_weight, gains
         )
-        totals, ry, rg = feed_and_reduce(count, table, x, att, lse, gains, cot, n, qkv, wqkv, ga, gb)
+        totals, ry, rg = feed_and_reduce(count, table, x, att, lse, gains, cot, n, qkv, wqkv, w2, ga, gb, *firsts)
         ry, rg = (rows.reshape(4, SLOTS, BLK, width) for rows in (ry, rg))
         return place_all(table, ry, rg, totals, blocks, part, layer_input.shape)
     else:

time: 196 us -> 193 us (0.985)
  Pallas kernels: 195 us -> 192 us
    pallas_call x1, Pallas kernels: 108 us -> 104 us  [feed_and_reduce(): pl.pallas_call(partial(rear_kernel, outer, inner), out_shape=tuple((jax.S...]
where the time goes in v2:
time: 193 us; the launch traced here: 192 us
  Pallas kernels  192 us (99%)
    pallas_call x1, Pallas kernels, feed_and_reduce(): pl.pallas_call(partial(rear_kernel, outer, inner), out_shape=tuple((jax.S...  104 us
    pallas_call x1, Pallas kernels, gather_and_attend(): pl.pallas_call(partial(front_kernel, outer, inner), out_shape=(shape((TAB...  79 us
    pallas_call x1, Pallas kernels, place_all(): pl.pallas_call(partial(place_kernel, part), out_shape=(out(block, ry.dtyp...  8.47 us

profile of v2, /device:TPU:0, one launch (start us, length us, event | category | flops | bytes accessed | tf_op | source)
XLA Modules:
  0.0 192.4 jit_solution(14026723636271591028)
XLA Ops:
  0.6 79.0 %gather_and_attend.1 = (s32[56,128]{1,0:T(8,128)}, f32[16,768]{1,0:T(8,128)}, bf16[640,768]{1,0:T(8,128)(2,1)}, bf16[640,768]{1,0:T(8,128)(2,1)}, bf16[688,768]{...) custom-call(s32[2,12]{1,0:T(2,128)} %refs_0_.1, ...), custom_call_target="tpu_custom_call" | custom-call | tf_op jit(solution)/shard_map/gather_and_attend/pallas_call | solution.py:1905
  79.7 104.1 %feed_and_reduce.1 = (f32[96,2048]{1,0:T(8,128)}, f32[96,2048]{1,0:T(8,128)}, f32[256,768]{1,0:T(8,128)}, f32[96,768]{1,0:T(8,128)}, f32[96,2304]{1,0:T(8,128)},...) custom-call(s32[56,128]{1,0:T(8,128)} %get-tuple-element.50.refs_0_.tab_ref, ...), custom_call_target="tpu_custom_call" | custom-call | tf_op jit(solution)/shard_map/feed_and_reduce/pallas_call | solution.py:2225
  183.8 8.5 %place_outputs.1 = (bf16[24,64,768]{2,1,0:T(8,128)(2,1)}, bf16[24,64,768]{2,1,0:T(8,128)(2,1)}, f32[96,768]{1,0:T(8,128)}, f32[96,768]{1,0:T(8,128)}, f32[96,768...) custom-call(s32[56,128]{1,0:T(8,128)} %get-tuple-element.50.refs_0_., ...), custom_call_target="tpu_custom_call" | custom-call | tf_op jit(solution)/shard_map/place_outputs/pallas_call | solution.py:2312

commit v3 on v2

--- a/solution.py
+++ b/solution.py
@@ -1509,11 +1509,11 @@
 
 
 def front_kernel(outer, inner, *refs):
-    (raw_ref, rows_any, cots_any, *weights), refs = refs[:9], refs[9:]
-    (wd_any, *gain_refs), refs = refs[:4], refs[4:]
+    (lens_ref, rows_any, cots_any, *weights), refs = refs[:9], refs[9:]
+    (wd_any, wc_ref), refs = refs[:2], refs[2:]
     (tab_ref, gains_ref), outs_any, (ga_ref, gb_ref), refs = refs[:2], refs[2:16], refs[16:18], refs[18:]
     (stage, lens_all, tabs, psend, precv, xsend, xrecv, rows_ref, cots_ref), refs = refs[:9], refs[9:]
-    (lens_ref, wd_ref, wc_ref), refs = refs[:3], refs[3:]
+    wd_ref, refs = refs[0], refs[1:]
     held, gc_ref, refs = refs[:14], refs[14], refs[15:]
     x_ref, cot_ref, n_ref, qkv_ref, att_ref, lse_ref, wqkv_ref, w2_ref, h1_ref, nt_ref, ntt_ref, b0_ref, b1_ref, b2_ref = held
     (l_send, l_recv, t_sem, w_sem, z_send, z_recv, y_send, y_recv, c_send, c_recv, d_send, d_recv, own_sem,
@@ -1548,22 +1548,6 @@
     for load in row_loads:
         load.start()
 
-    wc_ref[...] = jnp.zeros(wc_ref.shape, wc_ref.dtype)
-    for number, ref in enumerate(gain_refs):
-        wc_ref[number : number + 1, :part] = ref[...].reshape(1, part)
-    micro, spots = raw_ref.shape
-    lens_ref[...] = jnp.zeros(lens_ref.shape, lens_ref.dtype)
-    lens_ref[:micro, :spots] = raw_ref[...]
-    raw = lens_ref[...]
-    spread = jnp.zeros((1, 128), jnp.int32)
-    for device in range(4):
-        line = jnp.zeros((1, 128), jnp.int32)
-        for number in range(micro):
-            shift = device * micro * spots + number * spots
-            moved = raw if shift == 0 else pltpu.roll(raw, shift, 1)
-            line = line + moved[number : number + 1]
-        spread = jnp.where(rank == device, line, spread)
-    lens_ref[...] = jnp.broadcast_to(spread, (8, 128))
     links.greet(True)
     lens_all[rank] = lens_ref[...]
     for step in range(1, 4):
@@ -1892,7 +1876,7 @@
             copy.wait()
 
 
-def gather_and_attend(count, lens, rows, cots, weights, wd, gains):
+def gather_and_attend(count, lens, rows, cots, weights, wd, wc):
     outer, inner = grid_of(count)
     block = rows.shape[1:]
     part, hidden = weights[0].shape[0], weights[-1].shape[1]
@@ -1907,14 +1891,14 @@
         out_shape=(shape((TABLE_ROWS, 128), jnp.int32), shape((16, D), F32)) + held + (
             shape((count, part, hidden), BF16), shape((count,) + wd.shape, BF16),
         ),
-        in_specs=[VMEM] + [ANY] * 9 + [VMEM] * 3,
+        in_specs=[VMEM] + [ANY] * 9 + [VMEM],
         out_specs=(VMEM,) * 2 + (ANY,) * 16,
         scratch_shapes=[
             pltpu.VMEM((part, total), BF16), pltpu.VMEM((4, 8, 128), jnp.int32), pltpu.SMEM((TABLE_ROWS, 128), jnp.int32),
             pltpu.VMEM((2, 2, SLOTS) + block, BF16), pltpu.VMEM((2, 2, SLOTS) + block, BF16),
             pltpu.VMEM((2, SLOTS) + block, BF16), pltpu.VMEM((2, SLOTS) + block, BF16),
             pltpu.VMEM(rows.shape, BF16), pltpu.VMEM(cots.shape, BF16),
-            pltpu.VMEM((8, 128), jnp.int32), pltpu.VMEM(wd.shape, BF16), pltpu.VMEM((16, 128), BF16),
+            pltpu.VMEM(wd.shape, BF16),
             *(pltpu.VMEM(one.shape, one.dtype) for one in held), pltpu.VMEM((count, 16, 128), BF16),
             dma((3,)), dma((3,)), dma((1,)), dma((11,)),
             dma((2, outer - 1, kinds, 2)), dma((2, outer - 1, kinds, 2)), dma((outer, kinds)), dma((outer, kinds)),
@@ -1925,7 +1909,7 @@
             collective_id=1, has_side_effects=True, vmem_limit_bytes=VMEM_LIMIT
         ),
         name="gather_and_attend",
-    )(lens, rows, cots, *weights, wd, *gains)
+    )(lens, rows, cots, *weights, wd, wc)
 
 
 ACROSS_FIRST = (1, 2)
@@ -2236,8 +2220,8 @@
     return outs[:6], outs[6], outs[7]
 
 
-def place_kernel(part, tab_ref, ry_ref, rg_ref, og_ref, ou_ref, od_ref, oo_ref, op_ref, oc_ref, *refs):
-    (y_ref, g_ref, q_out, k_out, v_out, o_out, g_out, u_out, d_out, one_out, side_out, two_out), refs = refs[:12], refs[12:]
+def place_kernel(tab_ref, ry_ref, rg_ref, og_ref, ou_ref, od_ref, oo_ref, op_ref, oc_ref, *refs):
+    (y_ref, g_ref, q_out, k_out, v_out, o_out, g_out, u_out, d_out, gains_out), refs = refs[:10], refs[10:]
     (y_buf, g_buf, zero, bg, bu, bd, bo, bp, sem_in, sem_out, sem_rows, sem_home) = refs
     blocks = y_buf.shape[0]
     base = lax.axis_index("rep") * blocks
@@ -2266,8 +2250,7 @@
         return carry
 
     lax.fori_loop(0, blocks, fetch, 0)
-    for number, out in enumerate((one_out, side_out, two_out)):
-        out[...] = oc_ref[number, :part]
+    gains_out[...] = oc_ref[...]
     writes = []
     for number, (buf, dst) in enumerate(((bg, g_out), (bu, u_out), (bd, d_out), (bo, o_out))):
         reads[number].wait()
@@ -2308,19 +2291,18 @@
     og, ou, od, oo, op, oc = totals
     block = (blocks,) + ry.shape[2:]
     dma, vmem = pltpu.SemaphoreType.DMA, pltpu.VMEM
-    gain = out((part,), F32)
-    y, g, q, k, v, o, gate, up, down, one, side, two = pl.pallas_call(
-        partial(place_kernel, part),
+    y, g, q, k, v, o, gate, up, down, gains = pl.pallas_call(
+        place_kernel,
         out_shape=(out(block, ry.dtype), out(block, rg.dtype), out(oo.shape, F32), out(oo.shape, F32), out(oo.shape, F32),
-                   out(oo.shape, F32), out(og.shape, F32), out(ou.shape, F32), out(od.shape, F32), gain, gain, gain),
+                   out(oo.shape, F32), out(og.shape, F32), out(ou.shape, F32), out(od.shape, F32), out(oc.shape, F32)),
         in_specs=[SMEM] + [ANY] * 7 + [VMEM],
-        out_specs=(ANY,) * 9 + (VMEM,) * 3,
+        out_specs=(ANY,) * 9 + (VMEM,),
         scratch_shapes=[vmem(block, ry.dtype), vmem(block, rg.dtype), vmem(block[1:], ry.dtype)] + [vmem(t.shape, F32) for t in totals[:5]]
         + [dma((5,)), dma((13,)), dma((2, blocks)), dma((2, blocks))],
         compiler_params=pltpu.CompilerParams(vmem_limit_bytes=VMEM_LIMIT),
         name="place_outputs",
     )(table, ry, rg, og, ou, od, oo, op, oc)
-    return (y.reshape(shape), g.reshape(shape), one, side, q, k, v, o, two, gate, up, down)
+    return (y.reshape(shape), g.reshape(shape), gains[0, :part], gains[1, :part], q, k, v, o, gains[2, :part], gate, up, down)
 
 
 def per_device(count, layer_input, cotangent, lengths, attn_gain, global_gain, query_weight, key_weight,
@@ -2333,16 +2315,19 @@
     cots_in = cotangent.reshape(blocks, BLK, width)
     weights = (query_weight, key_weight, value_weight, out_weight, gate_weight, up_weight)
     gains = (attn_gain, global_gain, ffn_gain)
+    wc = jnp.pad(jnp.stack(gains), ((0, 13), (0, 128 - part)))
     if grid_of(count)[1] == 2 and part % 16 == 0:
+        lens = lax.dynamic_update_slice(
+            jnp.zeros((8, 128), jnp.int32), lengths.reshape(1, blocks), (0, lax.axis_index("rep") * blocks)
+        )
         table, gains, x, cot, n, qkv, att, lse, wqkv, w2, *firsts, ga, gb = gather_and_attend(
-            count, lengths, rows_in, cots_in, weights, down_weight, gains
+            count, lens, rows_in, cots_in, weights, down_weight, wc
         )
         totals, ry, rg = feed_and_reduce(count, table, x, att, lse, gains, cot, n, qkv, wqkv, w2, ga, gb, *firsts)
         ry, rg = (rows.reshape(4, SLOTS, BLK, width) for rows in (ry, rg))
         return place_all(table, ry, rg, totals, blocks, part, layer_input.shape)
     else:
         table = deal_table(lengths)
-        wc = jnp.pad(jnp.stack(gains), ((0, 13), (0, 128 - part)))
         splits = ((0, 4 * width), (4 * width, 2 * hidden))
         ga, gb, gc, rows, cots = gather_weights(
             count, splits, table, rows_in, cots_in, jnp.concatenate(weights, axis=1), down_weight, wc

time: 193 us -> 197 us (1.021)
  local copies, waits for them, and re-layouts: 0 us -> 2.75 us
where the time goes in v3:
time: 197 us
  Pallas kernels  192 us (97%)
  local copies, waits for them, and re-layouts  2.75 us (1%)
    pallas_call x1, Pallas kernels, feed_and_reduce(): pl.pallas_call(partial(rear_kernel, outer, inner), out_shape=tuple((jax.S...  104 us
    pallas_call x1, Pallas kernels, gather_and_attend(): pl.pallas_call(partial(front_kernel, outer, inner), out_shape=(shape((TAB...  79 us
    pallas_call x1, Pallas kernels, place_all(): pl.pallas_call(place_kernel, out_shape=(out(block, ry.dtype), out(block,...  8.73 us

profile of v3, /device:TPU:0, one launch (start us, length us, event | category | flops | bytes accessed | tf_op | source)
XLA Modules:
  0.0 196.5 jit_solution(1005831040384797681)
XLA Ops:
  0.6 0.8 reshape.54
  1.4 1.3 fusion.8.refs_10_
  2.7 0.1 dynamic_update_slice.3.refs_0_
  2.8 0.0 copy-start
  2.8 0.6 copy-done
  3.4 79.0 %gather_and_attend.1 = (s32[56,128]{1,0:T(8,128)}, f32[16,768]{1,0:T(8,128)}, bf16[640,768]{1,0:T(8,128)(2,1)}, bf16[640,768]{1,0:T(8,128)(2,1)}, bf16[688,768]{...) custom-call(s32[8,128]{1,0:T(8,128)} %copy-done, ...), custom_call_target="tpu_custom_call" | custom-call | tf_op jit(solution)/shard_map/gather_and_attend/pallas_call | solution.py:1889
  82.4 104.0 %feed_and_reduce.1 = (f32[96,2048]{1,0:T(8,128)}, f32[96,2048]{1,0:T(8,128)}, f32[256,768]{1,0:T(8,128)}, f32[96,768]{1,0:T(8,128)}, f32[96,2304]{1,0:T(8,128)},...) custom-call(s32[56,128]{1,0:T(8,128)} %get-tuple-element.48.refs_0_.tab_ref, ...), custom_call_target="tpu_custom_call" | custom-call | tf_op jit(solution)/shard_map/feed_and_reduce/pallas_call | solution.py:2209
  186.5 8.7 %place_outputs.1 = (bf16[24,64,768]{2,1,0:T(8,128)(2,1)}, bf16[24,64,768]{2,1,0:T(8,128)(2,1)}, f32[96,768]{1,0:T(8,128)}, f32[96,768]{1,0:T(8,128)}, f32[96,768...) custom-call(s32[56,128]{1,0:T(8,128)} %get-tuple-element.48.refs_0_., ...), custom_call_target="tpu_custom_call" | custom-call | tf_op jit(solution)/shard_map/place_outputs/pallas_call | solution.py:2294
  195.2 1.3 slice_bitcast_fusion
  (1 shorter events, 0.0 us)
Async XLA Ops:
  2.8 0.6 copy-start

commit v4 on v2

--- a/solution.py
+++ b/solution.py
@@ -1981,11 +1981,18 @@
         fetch(7, b1_any, b1_ref.at[:ROWS, :wide]), fetch(8, b2_any, b2_ref.at[:ROWS, :wide]),
     ]
     load_products = fetch(9, ntt_any, ntt_ref)
-    load_rest = [
-        fetch(10, nt_any, n_ref.at[:ROWS]), fetch(2, wf_any, wf_ref.at[:, :, :, early:]),
-        fetch(3, wd_any.at[wide:], wd_ref.at[wide:]), fetch(11, b0_any, b0_ref.at[:ROWS, :wide]),
-        fetch(12, h1_any, fa_ref.at[:ROWS]), fetch(4, x_any, x_ref), fetch(5, att_any, att_ref), fetch(13, w2_any, wf_ref.at[:, :, :, :early]),
-    ]
+    kept = {}
+
+    def load_rest():
+        kept["rest"] = [
+            fetch(10, nt_any, n_ref.at[:ROWS]), fetch(2, wf_any, wf_ref.at[:, :, :, early:]),
+            fetch(3, wd_any.at[wide:], wd_ref.at[wide:]), fetch(11, b0_any, b0_ref.at[:ROWS, :wide]),
+        ]
+        kept["late"] = [
+            fetch(12, h1_any, fa_ref.at[:ROWS]), fetch(13, w2_any, wf_ref.at[:, :, :, :early]),
+            fetch(4, x_any, x_ref), fetch(5, att_any, att_ref),
+        ]
+
     links.greet(later=True)
 
     def weight(start, size):
@@ -2012,11 +2019,12 @@
     h1_ref, dv_ref = fa_ref, fa_ref
     tiles = hidden // FF_TILE
     half = tiles // 2
-    kept = {}
 
     def enter():
         for load in load_first:
             load.wait()
+        load_products.wait()
+        load_rest()
         for tile in range(TILES):
             rows = pl.ds(tile * QT, QT)
             gres_ref[rows, :] = (ga_ref[rows, :].astype(F32) * valid[tile * QT : (tile + 1) * QT]).astype(BF16)
@@ -2030,10 +2038,9 @@
             return carry
 
         lax.fori_loop(0, half, step, 0)
-        load_products.wait()
 
     def second_half():
-        for load in load_rest:
+        for load in kept["rest"]:
             load.wait()
 
         def step(tile, carry):
@@ -2069,6 +2076,9 @@
         lax.fori_loop(0, tiles, step, 0)
 
     def outward():
+        for load in kept["late"]:
+            load.wait()
+
         def step(tile, carry):
             cols = pl.ds(pl.multiple_of(tile * group, 128), group)
             value = h1_ref[:ROWS, cols] + mm(b0_ref[:ROWS, :hidden], wd_ref[:, cols])

time: 193 us -> 192 us (level)
  no operation moved by 1% of the time
where the time goes in v4:
time: 192 us
  Pallas kernels  191 us (99%)
    pallas_call x1, Pallas kernels, feed_and_reduce(): pl.pallas_call(partial(rear_kernel, outer, inner), out_shape=tuple((jax.S...  104 us
    pallas_call x1, Pallas kernels, gather_and_attend(): pl.pallas_call(partial(front_kernel, outer, inner), out_shape=(shape((TAB...  79 us
    pallas_call x1, Pallas kernels, place_all(): pl.pallas_call(partial(place_kernel, part), out_shape=(out(block, ry.dtyp...  8.43 us

profile of v4, /device:TPU:0, one launch (start us, length us, event | category | flops | bytes accessed | tf_op | source)
XLA Modules:
  0.0 191.9 jit_solution(5367344555285904438)
XLA Ops:
  0.6 79.0 %gather_and_attend.1 = (s32[56,128]{1,0:T(8,128)}, f32[16,768]{1,0:T(8,128)}, bf16[640,768]{1,0:T(8,128)(2,1)}, bf16[640,768]{1,0:T(8,128)(2,1)}, bf16[688,768]{...) custom-call(s32[2,12]{1,0:T(2,128)} %refs_0_.1, ...), custom_call_target="tpu_custom_call" | custom-call | tf_op jit(solution)/shard_map/gather_and_attend/pallas_call | solution.py:1905
  79.7 103.6 %feed_and_reduce.1 = (f32[96,2048]{1,0:T(8,128)}, f32[96,2048]{1,0:T(8,128)}, f32[256,768]{1,0:T(8,128)}, f32[96,768]{1,0:T(8,128)}, f32[96,2304]{1,0:T(8,128)},...) custom-call(s32[56,128]{1,0:T(8,128)} %get-tuple-element.50.refs_0_.tab_ref, ...), custom_call_target="tpu_custom_call" | custom-call | tf_op jit(solution)/shard_map/feed_and_reduce/pallas_call | solution.py:2235
  183.3 8.4 %place_outputs.1 = (bf16[24,64,768]{2,1,0:T(8,128)(2,1)}, bf16[24,64,768]{2,1,0:T(8,128)(2,1)}, f32[96,768]{1,0:T(8,128)}, f32[96,768]{1,0:T(8,128)}, f32[96,768...) custom-call(s32[56,128]{1,0:T(8,128)} %get-tuple-element.50.refs_0_., ...), custom_call_target="tpu_custom_call" | custom-call | tf_op jit(solution)/shard_map/place_outputs/pallas_call | solution.py:2322
